TPU v7x, 128 devices: a whole 4x4x4 slice. The times are simulated.
128 devices in a mesh: gx: 8 (over x_lo, z), gy: 4 (over y), gz: 4 (over x_hi, core).
Axes of the slice: x: 4 (x_hi: 2, x_lo: 2; x = x_hi * 2 + x_lo), y: 4, z: 4, core: 2. Of those that a mesh axis runs over, the one named last changes fastest.
Arguments:
- inputs: bfloat16 [2560, 8192], P(('gx', 'gz'), 'gy'), may hold values from -6 to 6
- out_grad: bfloat16 [2560, 8192], P(('gx', 'gz'), 'gy'), may hold values from -6 to 6
- gate_weight: bfloat16 [8192, 16384], P('gy', ('gx', 'gz')), may hold values from -0.0625 to 0.0625
- up_weight: bfloat16 [8192, 16384], P('gy', ('gx', 'gz')), may hold values from -0.0625 to 0.0625
- down_weight: bfloat16 [16384, 8192], P(('gx', 'gz'), 'gy'), may hold values from -0.046875 to 0.046875
Outputs:
- in_grad: bfloat16 [2560, 8192], P(('gx', 'gz'), 'gy')
All inputs are finite; a program needn't handle non-finite values.
Results may differ from a plain program's by a relative error of at most 0.0049.
Values may be sent and summed in bfloat16 or wider, within the bound.
No kernel may reach another device: no remote copies, remote signals or barrier semaphores. Data moves between devices by JAX's collectives and lax.ppermute only.
A program may use at most 128 MiB of HBM per device.

v0:
```python
import jax
import jax.numpy as jnp
from jax import lax
from jax.experimental import pallas as pl
from jax.experimental.pallas import tpu as pltpu
from jax.sharding import Mesh, PartitionSpec as P

CHUNKS = (40, 40)
RING = 4
XZ = ("xh", "xl", "z")
ORDER = (2, 1, 3, 0)
LAST = (((1,), (1,)), ((), ()))
VMEM_LIMIT = 40 << 20


def place_of(axis):
    if axis == "x":
        return lax.axis_index("xh") * 2 + lax.axis_index("xl")
    return lax.axis_index(axis)


def shift(value, axis, step):
    if axis == "x":
        order = lambda i: (i % 2) * 2 + i // 2
        pairs = [(order(i), order((i + step) % RING)) for i in range(RING)]
        return lax.ppermute(value, ("xl", "xh"), pairs)
    return lax.ppermute(value, axis, [(i, (i + step) % RING) for i in range(RING)])


def gather(value, axis, dim):
    here = place_of(axis)
    shape = value.shape[:dim] + (RING,) + value.shape[dim:]
    filled = jnp.zeros(shape, value.dtype)
    for step in (1, 3, 2, 0):
        piece = value if step == 0 else shift(value, axis, step)
        filled = lax.dynamic_update_index_in_dim(filled, piece, (here - step) % RING, dim)
    return filled


def terms_kernel(place, in_ref, grad_ref, gate_a, gate_b, up_a, up_b, down_a, down_b, *outs):
    step = pl.program_id(0)
    half = outs[0].shape[0]
    cols = jnp.concatenate((gate_a[...], gate_b[...], up_a[...], up_b[...]), axis=1)
    pair = jnp.dot(in_ref[...], cols, preferred_element_type=jnp.float32)
    lines = jnp.concatenate((down_a[...], down_b[...]), axis=0)
    back = lax.dot_general(grad_ref[...], lines, LAST, preferred_element_type=jnp.float32)
    split = pair.shape[1]
    for k in range(RING):

        @pl.when(step == k)
        def _(k=k):
            for side in range(2):
                out = outs[2 * k + side]
                rows = slice(side * half, (side + 1) * half)
                out[:, :split] = pair[rows].astype(out.dtype)
                out[:, split:] = back[rows].astype(out.dtype)


def partial_terms(place, rows_in, rows_grad, gates, ups, downs):
    rows, width = rows_in.shape
    half = rows // 2
    cut = downs[0].shape[0] // RING
    wide = 2 * cut
    bf, f32 = jnp.bfloat16, jnp.float32
    types = (bf, bf, f32, bf, bf, f32, f32, f32)
    act = pl.BlockSpec(memory_space=pltpu.VMEM)
    cols = pl.BlockSpec((width, cut), lambda step, place: (0, place[step]))
    lines = pl.BlockSpec((cut, width), lambda step, place: (place[step], 0))
    grid_spec = pltpu.PrefetchScalarGridSpec(
        num_scalar_prefetch=1,
        grid=(RING,),
        in_specs=[act, act, cols, cols, cols, cols, lines, lines],
        out_specs=[pl.BlockSpec((half, 3 * wide), lambda step, place: (0, 0)) for _ in types],
    )
    return pl.pallas_call(
        terms_kernel,
        grid_spec=grid_spec,
        out_shape=[jax.ShapeDtypeStruct((half, 3 * wide), t) for t in types],
        cost_estimate=pl.CostEstimate(
            flops=2 * rows * width * 12 * wide, bytes_accessed=20 << 20, transcendentals=0
        ),
        compiler_params=pltpu.CompilerParams(vmem_limit_bytes=VMEM_LIMIT),
        name="terms",
    )(place, rows_in, rows_grad, *gates, *ups, *downs)


def back_kernel(place, *rest):
    pieces, cols, out_ref, held = rest[:8], rest[8:12], rest[12], rest[13]
    half = pieces[0].shape[0]
    cut = pieces[0].shape[1] // 4
    span = RING * cut

    @pl.when(pl.program_id(0) == 0)
    def _():
        for k in range(RING):
            at = pl.multiple_of(place[k] * cut, cut)
            for side in range(2):
                for part in range(4):
                    held[side * half : (side + 1) * half, pl.ds(at + part * span, cut)] = pieces[
                        2 * k + side
                    ][:, part * cut : (part + 1) * cut]

    out_ref[...] = lax.dot_general(
        held[...],
        jnp.concatenate([c[...] for c in cols], axis=1),
        LAST,
        preferred_element_type=jnp.float32,
    ).astype(out_ref.dtype)


def back_terms(place, pieces, gates, ups, rows_cut=512):
    half = pieces[0].shape[0]
    width, span = gates[0].shape
    grid_spec = pltpu.PrefetchScalarGridSpec(
        num_scalar_prefetch=1,
        grid=(width // rows_cut,),
        in_specs=[pl.BlockSpec(memory_space=pltpu.VMEM) for _ in pieces]
        + [pl.BlockSpec((rows_cut, span), lambda n, place: (n, 0)) for _ in range(4)],
        out_specs=pl.BlockSpec((2 * half, rows_cut), lambda n, place: (0, n)),
        scratch_shapes=[pltpu.VMEM((2 * half, 4 * span), jnp.bfloat16)],
    )
    return pl.pallas_call(
        back_kernel,
        grid_spec=grid_spec,
        out_shape=jax.ShapeDtypeStruct((2 * half, width), jnp.bfloat16),
        cost_estimate=pl.CostEstimate(
            flops=16 * half * width * span, bytes_accessed=14 << 20, transcendentals=0
        ),
        compiler_params=pltpu.CompilerParams(vmem_limit_bytes=VMEM_LIMIT),
        name="back",
    )(place, *pieces, *gates, *ups)


def narrow(value):
    return value.astype(jnp.bfloat16)


def local_grads(total):
    wide = total.shape[1] // 3
    gate, upper, hidden_grad = total[:, :wide], total[:, wide : 2 * wide], total[:, 2 * wide :]
    logistic = jax.nn.sigmoid(gate)
    gate_grad = hidden_grad * upper * logistic * (1.0 + gate * (1.0 - logistic))
    up_grad = hidden_grad * gate * logistic
    return narrow(jnp.concatenate((gate_grad, up_grad), axis=1))


def first_rows(own_in, own_grad):
    return gather(own_in, "z", 0), gather(own_grad, "x", 0)


def second_rows(some_in, some_grad, width):
    rows_in = gather(some_in, "x", 0).reshape(-1, width)
    return rows_in, gather(some_grad, "z", 1).reshape(-1, width)


def finish(place, terms, gates, ups, rows):
    far_t, far_b, right_t, right_b, left_t, left_b, own_t, own_b = terms
    far_t = shift(far_t, "y", 1)
    far_b = shift(far_b, "y", -1)
    right_b = shift(right_b, "y", 1)
    left_t = shift(left_t, "y", -1)
    right_t = shift(narrow(right_t + far_t), "y", 1)
    left_b = shift(narrow(left_b + far_b), "y", -1)
    top = local_grads(own_t + left_t + right_t)
    low = local_grads(own_b + right_b + left_b)
    from_left_t = shift(top, "y", 1)
    from_right_b = shift(low, "y", -1)
    from_left_b = shift(low, "y", 1)
    from_right_t = shift(top, "y", -1)
    far_top = shift(from_left_t, "y", 1)
    far_low = shift(from_right_b, "y", -1)
    pieces = (far_top, far_low, from_right_t, from_right_b, from_left_t, from_left_b, top, low)
    partial_value = back_terms(place, pieces, gates, ups)
    blocks = partial_value.reshape(RING * RING, rows, -1)
    crossed = lax.all_to_all(blocks, XZ, 0, 0)
    return narrow(crossed.astype(jnp.float32).sum(axis=0))


def swap(value):
    return lax.ppermute(value, "core", [(0, 1), (1, 0)])


def step_shards(inputs, out_grad, gate_weight, up_weight, down_weight):
    gates = (gate_weight, swap(gate_weight))
    ups = (up_weight, swap(up_weight))
    downs = (down_weight, swap(down_weight))
    width = gate_weight.shape[0]
    place = (lax.axis_index("y") + jnp.array(ORDER, jnp.int32)) % RING
    results = []
    at = 0
    some = terms = None
    for rows in CHUNKS:
        own_in = lax.slice_in_dim(inputs, at, at + rows)
        own_grad = lax.slice_in_dim(out_grad, at, at + rows)
        at += rows
        if some is not None:
            own_in, own_grad, *some = lax.optimization_barrier((own_in, own_grad, *some))
            filled = second_rows(*some, width)
            terms = partial_terms(place, *filled, gates, ups, downs)
        some = first_rows(own_in, own_grad)
        if terms is not None:
            *some, terms = lax.optimization_barrier((*some, terms))
            results.append(finish(place, terms, gates, ups, last))
        last = rows
    filled = second_rows(*some, width)
    terms = partial_terms(place, *filled, gates, ups, downs)
    results.append(finish(place, terms, gates, ups, rows))
    return jnp.concatenate(results, axis=0)


def solution(mesh):
    fine = Mesh(mesh.devices.reshape(2, 4, 4, 2, 2), ("xl", "z", "y", "xh", "core"))
    tokens = ("xl", "z", "xh", "core")
    return jax.shard_map(
        step_shards,
        mesh=fine,
        in_specs=(P(tokens, "y"), P(tokens, "y"), P("y", tokens), P("y", tokens), P(tokens, "y")),
        out_specs=P(tokens, "y"),
        check_vma=False,
    )
```

profile of v0, /device:TPU:0, one launch (start us, length us, event | category | flops | bytes accessed | tf_op | source)
XLA Modules:
  0.0 283.4 jit_solution(7027748536572756068)
XLA Ops:
  24.6 3.7 %collective-permute-done.9 = bf16[40,2048]{1,0:T(8,128)(2,1)S(1)} collective-permute-done((bf16[40,2048]{1,0:T(8,128)(2,1)S(1)}, bf16[40,2048]{1,0:T(8,128)(2,1)S(1)}, u32[]{:S(2)}, u32[]{:S(2)}) %collective-permute-start.9) | collective-permute-done | bytes 163872 | tf_op jit(solution)/shard_map/ppermute | solution.py:26
  30.1 5.1 %collective-permute-done.11 = bf16[40,2048]{1,0:T(8,128)(2,1)S(1)} collective-permute-done((bf16[40,2048]{1,0:T(8,128)(2,1)S(1)}, bf16[40,2048]{1,0:T(8,128)(2,1)S(1)}, u32[]{:S(2)}, u32[]{:S(2)}) %collective-permute-start.11) | collective-permute-done | bytes 163872 | tf_op jit(solution)/shard_map/ppermute | solution.py:26
  38.5 4.0 %collective-permute-done.7 = bf16[40,2048]{1,0:T(8,128)(2,1)S(1)} collective-permute-done((bf16[40,2048]{1,0:T(8,128)(2,1)S(1)}, bf16[40,2048]{1,0:T(8,128)(2,1)S(1)}, u32[]{:S(2)}, u32[]{:S(2)}) %collective-permute-start.7) | collective-permute-done | bytes 163872 | tf_op jit(solution)/shard_map/ppermute | solution.py:27
  46.3 10.6 %collective-permute-done.15 = bf16[4,40,2048]{2,1,0:T(8,128)(2,1)S(1)} collective-permute-done((bf16[4,40,2048]{2,1,0:T(8,128)(2,1)S(1)}, bf16[4,40,2048]{2,1,0:T(8,128)(2,1)S(1)}, u32[]{:S(2)}, u32[]{:S(2)}) %collective-permute-start.15) | collective-permute-done | bytes 655392 | tf_op jit(solution)/shard_map/ppermute | solution.py:27
  58.9 12.1 %collective-permute-done.16 = bf16[4,40,2048]{2,1,0:T(8,128)(2,1)S(1)} collective-permute-done((bf16[4,40,2048]{2,1,0:T(8,128)(2,1)S(1)}, bf16[4,40,2048]{2,1,0:T(8,128)(2,1)S(1)}, u32[]{:S(2)}, u32[]{:S(2)}) %collective-permute-start.16) | collective-permute-done | bytes 655392 | tf_op jit(solution)/shard_map/ppermute | solution.py:27
  71.1 3.3 %collective-permute-start.13 = (bf16[4,40,2048]{2,1,0:T(8,128)(2,1)S(1)}, bf16[4,40,2048]{2,1,0:T(8,128)(2,1)S(1)}, u32[]{:S(2)}, u32[]{:S(2)}) collective-permute-start(bf16[4,40,2048]{2,1,0:T(8,128)(2,1)S(1)} %bitcast_dynamic-update-slice_fusion.28), channel_id=1, source_target_pairs={{0,66},{64,0},{2,64},{66,2},{1,67},{65,1},{3,65},{67,3},{4,70},{68... | collective-permute-start | bytes 1966088 | tf_op jit(solution)/shard_map/ppermute | solution.py:26
  74.5 12.3 %collective-permute-done.12 = bf16[4,40,2048]{2,1,0:T(8,128)(2,1)S(1)} collective-permute-done((bf16[4,40,2048]{2,1,0:T(8,128)(2,1)S(1)}, bf16[4,40,2048]{2,1,0:T(8,128)(2,1)S(1)}, u32[]{:S(2)}, u32[]{:S(2)}) %collective-permute-start.12) | collective-permute-done | bytes 655392 | tf_op jit(solution)/shard_map/ppermute | solution.py:26
  87.7 9.3 %collective-permute-done.13 = bf16[4,40,2048]{2,1,0:T(8,128)(2,1)S(1)} collective-permute-done((bf16[4,40,2048]{2,1,0:T(8,128)(2,1)S(1)}, bf16[4,40,2048]{2,1,0:T(8,128)(2,1)S(1)}, u32[]{:S(2)}, u32[]{:S(2)}) %collective-permute-start.13) | collective-permute-done | bytes 655392 | tf_op jit(solution)/shard_map/ppermute | solution.py:26
  101.2 14.2 %terms.2 = (bf16[320,768]{1,0:T(8,128)(2,1)S(1)}, bf16[320,768]{1,0:T(8,128)(2,1)S(1)}, f32[320,768]{1,0:T(8,128)S(1)}, bf16[320,768]{1,0:T(8,128)(2,1)S(1)}, bf...) custom-call(s32[4]{0:T(128)S(1)} %and_select_fusion.place, ...), custom_call_target="tpu_custom_call" | custom-call | flops 8053063680 | bytes 20971520 | tf_op jit(solution)/shard_map/terms/pallas_call | solution.py:75
  118.5 4.5 %collective-permute-start.36 = (bf16[4,40,2048]{2,1,0:T(8,128)(2,1)S(1)}, bf16[4,40,2048]{2,1,0:T(8,128)(2,1)S(1)}, u32[]{:S(2)}, u32[]{:S(2)}) collective-permute-start(bf16[4,40,2048]{2,1,0:T(8,128)(2,1)S(1)} %bitcast_dynamic-update-slice_fusion.16), channel_id=1, source_target_pairs={{0,16},{16,32},{32,48},{48,0},{1,17},{17,33},{33,49},{49,1},{2,18}... | collective-permute-start | bytes 1966088 | tf_op jit(solution)/shard_map/ppermute | solution.py:27
  126.0 4.4 %collective-permute-done.22 = bf16[320,768]{1,0:T(8,128)(2,1)S(1)} collective-permute-done((bf16[320,768]{1,0:T(8,128)(2,1)S(1)}, bf16[320,768]{1,0:T(8,128)(2,1)S(1)}, u32[]{:S(2)}, u32[]{:S(2)}) %collective-permute-start.22) | collective-permute-done | bytes 491552 | tf_op jit(solution)/shard_map/ppermute | solution.py:27
  134.3 3.9 %collective-permute-done.38 = bf16[4,40,2048]{2,1,0:T(8,128)(2,1)S(1)} collective-permute-done((bf16[4,40,2048]{2,1,0:T(8,128)(2,1)S(1)}, bf16[4,40,2048]{2,1,0:T(8,128)(2,1)S(1)}, u32[]{:S(2)}, u32[]{:S(2)}) %collective-permute-start.38) | collective-permute-done | bytes 655392 | tf_op jit(solution)/shard_map/ppermute | solution.py:27
  138.1 3.2 %collective-permute-start.21 = (bf16[320,768]{1,0:T(8,128)(2,1)S(1)}, bf16[320,768]{1,0:T(8,128)(2,1)S(1)}, u32[]{:S(2)}, u32[]{:S(2)}) collective-permute-start(bf16[320,768]{1,0:T(8,128)(2,1)S(1)} %get-tuple-element.48), channel_id=1, source_target_pairs={{0,12},{4,0},{8,4},{12,8},{1,13},{5,1},{9,5},{13,9},{2,14},{6,2},{... | collective-permute-start | bytes 1474568 | tf_op jit(solution)/shard_map/ppermute | solution.py:27
  141.5 8.4 %collective-permute-done.33 = bf16[4,40,2048]{2,1,0:T(8,128)(2,1)S(1)} collective-permute-done((bf16[4,40,2048]{2,1,0:T(8,128)(2,1)S(1)}, bf16[4,40,2048]{2,1,0:T(8,128)(2,1)S(1)}, u32[]{:S(2)}, u32[]{:S(2)}) %collective-permute-start.33) | collective-permute-done | bytes 655392 | tf_op jit(solution)/shard_map/ppermute | solution.py:26
  154.1 14.2 %terms.3 = (bf16[320,768]{1,0:T(8,128)(2,1)S(1)}, bf16[320,768]{1,0:T(8,128)(2,1)S(1)}, f32[320,768]{1,0:T(8,128)S(1)}, bf16[320,768]{1,0:T(8,128)(2,1)S(1)}, bf...) custom-call(s32[4]{0:T(128)S(1)} %and_select_fusion.place, ...), custom_call_target="tpu_custom_call" | custom-call | flops 8053063680 | bytes 20971520 | tf_op jit(solution)/shard_map/terms/pallas_call | solution.py:75
  173.5 9.0 %collective-permute-done.45 = bf16[320,768]{1,0:T(8,128)(2,1)S(1)} collective-permute-done((bf16[320,768]{1,0:T(8,128)(2,1)S(1)}, bf16[320,768]{1,0:T(8,128)(2,1)S(1)}, u32[]{:S(2)}, u32[]{:S(2)}) %collective-permute-start.45) | collective-permute-done | bytes 491552 | tf_op jit(solution)/shard_map/ppermute | solution.py:27
  185.0 4.6 %collective-permute-done.29.rest_3_ = bf16[320,512]{1,0:T(8,128)(2,1)S(1)} collective-permute-done((bf16[320,512]{1,0:T(8,128)(2,1)S(1)}, bf16[320,512]{1,0:T(8,128)(2,1)S(1)}, u32[]{:S(2)}, u32[]{:S(2)}) %collective-permute-start.29) | collective-permute-done | bytes 327712 | tf_op jit(solution)/shard_map/ppermute | solution.py:27
  195.0 6.1 %collective-permute-done.32.rest_5_ = bf16[320,512]{1,0:T(8,128)(2,1)S(1)} collective-permute-done((bf16[320,512]{1,0:T(8,128)(2,1)S(1)}, bf16[320,512]{1,0:T(8,128)(2,1)S(1)}, u32[]{:S(2)}, u32[]{:S(2)}) %collective-permute-start.32) | collective-permute-done | bytes 327712 | tf_op jit(solution)/shard_map/ppermute | solution.py:27
  206.3 8.5 %back.2 = bf16[640,2048]{1,0:T(8,128)(2,1)} custom-call(s32[4]{0:T(128)S(1)} %and_select_fusion.place, bf16[320,512]{1,0:T(8,128)(2,1)S(1)} %collective-permute-done.25.rest_0_, bf16[320,512]{1,0:T(8,128)(2,1)S(1)} %collective-permute-done.30.rest_1_, bf16[320,512]{1,0:T(8,128)(2,1)S(1)} %collective-permute-done.31.rest_2_, ...), custom_call_target="tpu_custom_call" | custom-call | flops 5368709120 | bytes 14680064 | tf_op jit(solution)/shard_map/back/pallas_call | solution.py:122
  214.9 8.7 %all-to-all-start = ((bf16[16,40,2048]{2,1,0:T(8,128)(2,1)}), bf16[16,40,2048]{2,1,0:T(8,128)(2,1)}, u32[]{:S(2)}, u32[]{:S(2)}) async-start(bf16[16,40,2048]{2,1,0:T(8,128)(2,1)} %bitcast.30), calls=%async_computation | async-start | bytes 5242880 | tf_op jit(solution)/shard_map/all_to_all | solution.py:175
  240.2 3.4 %collective-permute-done.43.rest_0_ = bf16[320,512]{1,0:T(8,128)(2,1)S(1)} collective-permute-done((bf16[320,512]{1,0:T(8,128)(2,1)S(1)}, bf16[320,512]{1,0:T(8,128)(2,1)S(1)}, u32[]{:S(2)}, u32[]{:S(2)}) %collective-permute-start.43) | collective-permute-done | bytes 327712 | tf_op jit(solution)/shard_map/ppermute | solution.py:27
  243.6 8.6 %back.3 = bf16[640,2048]{1,0:T(8,128)(2,1)} custom-call(s32[4]{0:T(128)S(1)} %and_select_fusion.place, bf16[320,512]{1,0:T(8,128)(2,1)S(1)} %collective-permute-done.43.rest_0_, bf16[320,512]{1,0:T(8,128)(2,1)S(1)} %collective-permute-done.48.rest_1_, bf16[320,512]{1,0:T(8,128)(2,1)S(1)} %collective-permute-done.49.rest_2_, ...), custom_call_target="tpu_custom_call" | custom-call | flops 5368709120 | bytes 14680064 | tf_op jit(solution)/shard_map/back/pallas_call | solution.py:122
  252.2 8.1 %all-to-all-start.1 = ((bf16[16,40,2048]{2,1,0:T(8,128)(2,1)}), bf16[16,40,2048]{2,1,0:T(8,128)(2,1)S(1)}, u32[]{:S(2)}, u32[]{:S(2)}) async-start(bf16[16,40,2048]{2,1,0:T(8,128)(2,1)} %bitcast.44), calls=%async_computation.1 | async-start | bytes 5242880 | tf_op jit(solution)/shard_map/all_to_all | solution.py:175
  262.5 19.6 %all-to-all-done.1 = bf16[16,40,2048]{2,1,0:T(8,128)(2,1)S(1)} async-done(((bf16[16,40,2048]{2,1,0:T(8,128)(2,1)}), bf16[16,40,2048]{2,1,0:T(8,128)(2,1)S(1)}, u32[]{:S(2)}, u32[]{:S(2)}) %all-to-all-start.1) | async-done | bytes 2621472 | tf_op jit(solution)/shard_map/all_to_all | solution.py:175
  (186 shorter events, 92.9 us)
Async XLA Ops:
  15.8 83.3 %collective-permute-start.18 = (bf16[2048,512]{1,0:T(8,128)(2,1)}, bf16[2048,512]{1,0:T(8,128)(2,1)S(1)}, u32[]{:S(2)}, u32[]{:S(2)}) collective-permute-start(bf16[2048,512]{1,0:T(8,128)(2,1)} %rest_8_.3), channel_id=1, source_target_pairs={{0,1},{1,0},{2,3},{3,2},{4,5},{5,4},{6,7},{7,6},{8,9},{9,8},{10,11... | collective-permute-start | bytes 6291464 | tf_op jit(solution)/shard_map/ppermute | solution.py:180
  16.8 82.3 %collective-permute-start.19 = (bf16[2048,512]{1,0:T(8,128)(2,1)S(1)}, bf16[2048,512]{1,0:T(8,128)(2,1)S(1)}, u32[]{:S(2)}, u32[]{:S(2)}) collective-permute-start(bf16[2048,512]{1,0:T(8,128)(2,1)S(1)} %copy-done.2), channel_id=1, source_target_pairs={{0,1},{1,0},{2,3},{3,2},{4,5},{5,4},{6,7},{7,6},{8,9},{9,8},{10,11... | collective-permute-start | bytes 6291464 | tf_op jit(solution)/shard_map/ppermute | solution.py:180
  18.4 80.8 %collective-permute-start.20 = (bf16[512,2048]{1,0:T(8,128)(2,1)}, bf16[512,2048]{1,0:T(8,128)(2,1)S(1)}, u32[]{:S(2)}, u32[]{:S(2)}) collective-permute-start(bf16[512,2048]{1,0:T(8,128)(2,1)} %down_a.3), channel_id=1, source_target_pairs={{0,1},{1,0},{2,3},{3,2},{4,5},{5,4},{6,7},{7,6},{8,9},{9,8},{10,11... | collective-permute-start | bytes 6291464 | tf_op jit(solution)/shard_map/ppermute | solution.py:180
  46.3 24.7 %collective-permute-start.16 = (bf16[4,40,2048]{2,1,0:T(8,128)(2,1)S(1)}, bf16[4,40,2048]{2,1,0:T(8,128)(2,1)S(1)}, u32[]{:S(2)}, u32[]{:S(2)}) collective-permute-start(bf16[4,40,2048]{2,1,0:T(8,128)(2,1)S(1)} %bitcast_dynamic-update-slice_fusion.24), channel_id=1, source_target_pairs={{0,48},{16,0},{32,16},{48,32},{1,49},{17,1},{33,17},{49,33},{2,50}... | collective-permute-start | bytes 1966088 | tf_op jit(solution)/shard_map/ppermute | solution.py:27
  71.0 15.9 %collective-permute-start.12 = (bf16[4,40,2048]{2,1,0:T(8,128)(2,1)S(1)}, bf16[4,40,2048]{2,1,0:T(8,128)(2,1)S(1)}, u32[]{:S(2)}, u32[]{:S(2)}) collective-permute-start(bf16[4,40,2048]{2,1,0:T(8,128)(2,1)S(1)} %bitcast_dynamic-update-slice_fusion.28), channel_id=1, source_target_pairs={{0,64},{64,2},{2,66},{66,0},{1,65},{65,3},{3,67},{67,1},{4,68},{68... | collective-permute-start | bytes 1966088 | tf_op jit(solution)/shard_map/ppermute | solution.py:26
  71.1 25.9 %collective-permute-start.13 = (bf16[4,40,2048]{2,1,0:T(8,128)(2,1)S(1)}, bf16[4,40,2048]{2,1,0:T(8,128)(2,1)S(1)}, u32[]{:S(2)}, u32[]{:S(2)}) collective-permute-start(bf16[4,40,2048]{2,1,0:T(8,128)(2,1)S(1)} %bitcast_dynamic-update-slice_fusion.28), channel_id=1, source_target_pairs={{0,66},{64,0},{2,64},{66,2},{1,67},{65,1},{3,65},{67,3},{4,70},{68... | collective-permute-start | bytes 1966088 | tf_op jit(solution)/shard_map/ppermute | solution.py:26
  125.1 24.8 %collective-permute-start.33 = (bf16[4,40,2048]{2,1,0:T(8,128)(2,1)S(1)}, bf16[4,40,2048]{2,1,0:T(8,128)(2,1)S(1)}, u32[]{:S(2)}, u32[]{:S(2)}) collective-permute-start(bf16[4,40,2048]{2,1,0:T(8,128)(2,1)S(1)} %bitcast_dynamic-update-slice_fusion.20), channel_id=1, source_target_pairs={{0,64},{64,2},{2,66},{66,0},{1,65},{65,3},{3,67},{67,1},{4,68},{68... | collective-permute-start | bytes 1966088 | tf_op jit(solution)/shard_map/ppermute | solution.py:26
  130.4 19.9 %collective-permute-start.34 = (bf16[4,40,2048]{2,1,0:T(8,128)(2,1)S(1)}, bf16[4,40,2048]{2,1,0:T(8,128)(2,1)S(1)}, u32[]{:S(2)}, u32[]{:S(2)}) collective-permute-start(bf16[4,40,2048]{2,1,0:T(8,128)(2,1)S(1)} %bitcast_dynamic-update-slice_fusion.20), channel_id=1, source_target_pairs={{0,66},{64,0},{2,64},{66,2},{1,67},{65,1},{3,65},{67,3},{4,70},{68... | collective-permute-start | bytes 1966088 | tf_op jit(solution)/shard_map/ppermute | solution.py:26
  131.3 21.2 %collective-permute-start.35 = (bf16[4,40,2048]{2,1,0:T(8,128)(2,1)S(1)}, bf16[4,40,2048]{2,1,0:T(8,128)(2,1)S(1)}, u32[]{:S(2)}, u32[]{:S(2)}) collective-permute-start(bf16[4,40,2048]{2,1,0:T(8,128)(2,1)S(1)} %bitcast_dynamic-update-slice_fusion.20), channel_id=1, source_target_pairs={{0,2},{64,66},{2,0},{66,64},{1,3},{65,67},{3,1},{67,65},{4,6},{68,... | collective-permute-start | bytes 1966088 | tf_op jit(solution)/shard_map/ppermute | solution.py:26
  133.6 36.0 %collective-permute-start.26 = (bf16[320,768]{1,0:T(8,128)(2,1)S(1)}, bf16[320,768]{1,0:T(8,128)(2,1)S(1)}, u32[]{:S(2)}, u32[]{:S(2)}) collective-permute-start(bf16[320,768]{1,0:T(8,128)(2,1)S(1)} %get-tuple-element.52), channel_id=1, source_target_pairs={{0,4},{4,8},{8,12},{12,0},{1,5},{5,9},{9,13},{13,1},{2,6},{6,10},{... | collective-permute-start | bytes 1474568 | tf_op jit(solution)/shard_map/ppermute | solution.py:27
  138.1 33.2 %collective-permute-start.21 = (bf16[320,768]{1,0:T(8,128)(2,1)S(1)}, bf16[320,768]{1,0:T(8,128)(2,1)S(1)}, u32[]{:S(2)}, u32[]{:S(2)}) collective-permute-start(bf16[320,768]{1,0:T(8,128)(2,1)S(1)} %get-tuple-element.48), channel_id=1, source_target_pairs={{0,12},{4,0},{8,4},{12,8},{1,13},{5,1},{9,5},{13,9},{2,14},{6,2},{... | collective-permute-start | bytes 1474568 | tf_op jit(solution)/shard_map/ppermute | solution.py:27
  149.9 19.7 %collective-permute-start.28 = (bf16[320,768]{1,0:T(8,128)(2,1)}, bf16[320,768]{1,0:T(8,128)(2,1)S(1)}, u32[]{:S(2)}, u32[]{:S(2)}) collective-permute-start(bf16[320,768]{1,0:T(8,128)(2,1)} %add_convert_fusion.2), channel_id=1, source_target_pairs={{0,12},{4,0},{8,4},{12,8},{1,13},{5,1},{9,5},{13,9},{2,14},{6,2},{... | collective-permute-start | bytes 1474568 | tf_op jit(solution)/shard_map/ppermute | solution.py:27
  150.3 21.0 %collective-permute-start.23 = (bf16[320,768]{1,0:T(8,128)(2,1)}, bf16[320,768]{1,0:T(8,128)(2,1)S(1)}, u32[]{:S(2)}, u32[]{:S(2)}) collective-permute-start(bf16[320,768]{1,0:T(8,128)(2,1)} %add_convert_fusion.3), channel_id=1, source_target_pairs={{0,4},{4,8},{8,12},{12,0},{1,5},{5,9},{9,13},{13,1},{2,6},{6,10},{... | collective-permute-start | bytes 1474568 | tf_op jit(solution)/shard_map/ppermute | solution.py:27
  170.0 19.6 %collective-permute-start.29 = (bf16[320,512]{1,0:T(8,128)(2,1)S(1)}, bf16[320,512]{1,0:T(8,128)(2,1)S(1)}, u32[]{:S(2)}, u32[]{:S(2)}) collective-permute-start(bf16[320,512]{1,0:T(8,128)(2,1)S(1)} %pad_maximum_fusion.1.rest_7_), channel_id=1, source_target_pairs={{0,12},{4,0},{8,4},{12,8},{1,13},{5,1},{9,5},{13,9},{2,14},{6,2},{... | collective-permute-start | bytes 983048 | tf_op jit(solution)/shard_map/ppermute | solution.py:27
  171.7 20.3 %collective-permute-start.24 = (bf16[320,512]{1,0:T(8,128)(2,1)S(1)}, bf16[320,512]{1,0:T(8,128)(2,1)S(1)}, u32[]{:S(2)}, u32[]{:S(2)}) collective-permute-start(bf16[320,512]{1,0:T(8,128)(2,1)S(1)} %pad_maximum_fusion.rest_6_), channel_id=1, source_target_pairs={{0,4},{4,8},{8,12},{12,0},{1,5},{5,9},{9,13},{13,1},{2,6},{6,10},{... | collective-permute-start | bytes 983048 | tf_op jit(solution)/shard_map/ppermute | solution.py:27
  172.5 21.6 %collective-permute-start.40 = (bf16[320,768]{1,0:T(8,128)(2,1)S(1)}, bf16[320,768]{1,0:T(8,128)(2,1)S(1)}, u32[]{:S(2)}, u32[]{:S(2)}) collective-permute-start(bf16[320,768]{1,0:T(8,128)(2,1)S(1)} %get-tuple-element.60), channel_id=1, source_target_pairs={{0,4},{4,8},{8,12},{12,0},{1,5},{5,9},{9,13},{13,1},{2,6},{6,10},{... | collective-permute-start | bytes 1474568 | tf_op jit(solution)/shard_map/ppermute | solution.py:27
  173.3 27.8 %collective-permute-start.32 = (bf16[320,512]{1,0:T(8,128)(2,1)S(1)}, bf16[320,512]{1,0:T(8,128)(2,1)S(1)}, u32[]{:S(2)}, u32[]{:S(2)}) collective-permute-start(bf16[320,512]{1,0:T(8,128)(2,1)S(1)} %pad_maximum_fusion.1.rest_7_), channel_id=1, source_target_pairs={{0,4},{4,8},{8,12},{12,0},{1,5},{5,9},{9,13},{13,1},{2,6},{6,10},{... | collective-permute-start | bytes 983048 | tf_op jit(solution)/shard_map/ppermute | solution.py:27
  182.5 18.6 %collective-permute-start.31 = (bf16[320,512]{1,0:T(8,128)(2,1)S(1)}, bf16[320,512]{1,0:T(8,128)(2,1)S(1)}, u32[]{:S(2)}, u32[]{:S(2)}) collective-permute-start(bf16[320,512]{1,0:T(8,128)(2,1)S(1)} %pad_maximum_fusion.rest_6_), channel_id=1, source_target_pairs={{0,12},{4,0},{8,4},{12,8},{1,13},{5,1},{9,5},{13,9},{2,14},{6,2},{... | collective-permute-start | bytes 983048 | tf_op jit(solution)/shard_map/ppermute | solution.py:27
  194.1 29.5 %collective-permute-start.44 = (bf16[320,768]{1,0:T(8,128)(2,1)S(1)}, bf16[320,768]{1,0:T(8,128)(2,1)}, u32[]{:S(2)}, u32[]{:S(2)}) collective-permute-start(bf16[320,768]{1,0:T(8,128)(2,1)S(1)} %get-tuple-element.62), channel_id=1, source_target_pairs={{0,4},{4,8},{8,12},{12,0},{1,5},{5,9},{9,13},{13,1},{2,6},{6,10},{... | collective-permute-start | bytes 1474568 | tf_op jit(solution)/shard_map/ppermute | solution.py:27
  201.1 24.3 %collective-permute-start.39 = (bf16[320,768]{1,0:T(8,128)(2,1)S(1)}, bf16[320,768]{1,0:T(8,128)(2,1)S(1)}, u32[]{:S(2)}, u32[]{:S(2)}) collective-permute-start(bf16[320,768]{1,0:T(8,128)(2,1)S(1)} %get-tuple-element.58), channel_id=1, source_target_pairs={{0,12},{4,0},{8,4},{12,8},{1,13},{5,1},{9,5},{13,9},{2,14},{6,2},{... | collective-permute-start | bytes 1474568 | tf_op jit(solution)/shard_map/ppermute | solution.py:27
  201.1 22.5 %collective-permute-start.46 = (bf16[320,768]{1,0:T(8,128)(2,1)}, bf16[320,768]{1,0:T(8,128)(2,1)}, u32[]{:S(2)}, u32[]{:S(2)}) collective-permute-start(bf16[320,768]{1,0:T(8,128)(2,1)} %add_convert_fusion), channel_id=1, source_target_pairs={{0,12},{4,0},{8,4},{12,8},{1,13},{5,1},{9,5},{13,9},{2,14},{6,2},{... | collective-permute-start | bytes 1474568 | tf_op jit(solution)/shard_map/ppermute | solution.py:27
  202.3 23.1 %collective-permute-start.41 = (bf16[320,768]{1,0:T(8,128)(2,1)}, bf16[320,768]{1,0:T(8,128)(2,1)}, u32[]{:S(2)}, u32[]{:S(2)}) collective-permute-start(bf16[320,768]{1,0:T(8,128)(2,1)} %add_convert_fusion.1), channel_id=1, source_target_pairs={{0,4},{4,8},{8,12},{12,0},{1,5},{5,9},{9,13},{13,1},{2,6},{6,10},{... | collective-permute-start | bytes 1474568 | tf_op jit(solution)/shard_map/ppermute | solution.py:27
  214.9 37.3 %all-to-all-start = ((bf16[16,40,2048]{2,1,0:T(8,128)(2,1)}), bf16[16,40,2048]{2,1,0:T(8,128)(2,1)}, u32[]{:S(2)}, u32[]{:S(2)}) async-start(bf16[16,40,2048]{2,1,0:T(8,128)(2,1)} %bitcast.30), calls=%async_computation | async-start | bytes 5242880 | tf_op jit(solution)/shard_map/all_to_all | solution.py:175
  252.2 29.9 %all-to-all-start.1 = ((bf16[16,40,2048]{2,1,0:T(8,128)(2,1)}), bf16[16,40,2048]{2,1,0:T(8,128)(2,1)S(1)}, u32[]{:S(2)}, u32[]{:S(2)}) async-start(bf16[16,40,2048]{2,1,0:T(8,128)(2,1)} %bitcast.44), calls=%async_computation.1 | async-start | bytes 5242880 | tf_op jit(solution)/shard_map/all_to_all | solution.py:175
  (48 other events, 748.3 us)
where the time goes:
time: 284 us; the launch traced here: 283 us
  waiting for transfers between devices  135 us (48%)
  starting transfers between devices  76.8 us (27%)
  Pallas kernels  45.5 us (16%)
  local copies, waits for them, and re-layouts  14.6 us (5%)
  other arithmetic  11 us (4%)
    ppermute x36, waiting for transfers between devices, shift(): lax.ppermute(value, axis, [(i, (i + step) % RING) for i in range(RING)])  74.5 us
    ppermute x36, starting transfers between devices, shift(): lax.ppermute(value, axis, [(i, (i + step) % RING) for i in range(RING)])  46.2 us
    ppermute x12, waiting for transfers between devices, shift(): return lax.ppermute(value, ('xl', 'xh'), pairs)  40.7 us
    pallas_call x2, Pallas kernels, partial_terms(): pl.pallas_call(terms_kernel, grid_spec=grid_spec, out_shape=[jax.ShapeDty...  28.4 us
    all_to_all x2, waiting for transfers between devices, finish(): crossed = lax.all_to_all(blocks, XZ, 0, 0)  19.6 us
    pallas_call x2, Pallas kernels, back_terms(): pl.pallas_call(back_kernel, grid_spec=grid_spec, out_shape=jax.ShapeDtype...  17.1 us
    all_to_all x2, starting transfers between devices, finish(): crossed = lax.all_to_all(blocks, XZ, 0, 0)  16.8 us
    ppermute x12, starting transfers between devices, shift(): return lax.ppermute(value, ('xl', 'xh'), pairs)  13.1 us
  transfers between devices with their start and end apart: 53, of which 26 were waited for; matrix products, arithmetic and copies ran while one was open for 7% of the time, Pallas kernels for 11%

commit v1 on v0

--- a/solution.py
+++ b/solution.py
@@ -1,3 +1,5 @@
+import functools
+
 import jax
 import jax.numpy as jnp
 from jax import lax
@@ -27,61 +29,142 @@
     return lax.ppermute(value, axis, [(i, (i + step) % RING) for i in range(RING)])
 
 
-def gather(value, axis, dim):
-    here = place_of(axis)
-    shape = value.shape[:dim] + (RING,) + value.shape[dim:]
-    filled = jnp.zeros(shape, value.dtype)
-    for step in (1, 3, 2, 0):
-        piece = value if step == 0 else shift(value, axis, step)
-        filled = lax.dynamic_update_index_in_dim(filled, piece, (here - step) % RING, dim)
-    return filled
-
-
-def terms_kernel(place, in_ref, grad_ref, gate_a, gate_b, up_a, up_b, down_a, down_b, *outs):
+def around(value, axis):
+    return [value] + [shift(value, axis, step) for step in range(1, RING)]
+
+
+def join_kernel(rows, place, *refs):
+    pieces, outs = refs[:RING], refs[RING:]
+    for k in range(RING):
+        at = 0
+        for count, out in zip(rows, outs):
+            to = pl.multiple_of(place[k] * count, count)
+            out[pl.ds(to, count)] = pieces[k][at : at + count]
+            at += count
+
+
+def join(axis, pieces):
+    width = pieces[0].shape[1]
+    place = (place_of(axis) - jnp.arange(RING, dtype=jnp.int32)) % RING
+    spec = pl.BlockSpec(memory_space=pltpu.VMEM)
+    return pl.pallas_call(
+        functools.partial(join_kernel, CHUNKS),
+        in_specs=[pl.BlockSpec(memory_space=pltpu.SMEM)] + [spec] * RING,
+        out_specs=[spec] * len(CHUNKS),
+        out_shape=[jax.ShapeDtypeStruct((RING * rows, width), pieces[0].dtype) for rows in CHUNKS],
+        cost_estimate=pl.CostEstimate(flops=1 << 20, bytes_accessed=3 << 20, transcendentals=0),
+        compiler_params=pltpu.CompilerParams(vmem_limit_bytes=16 << 20),
+        name="join",
+    )(place, *pieces)
+
+
+def assemble(axis_place, pieces, held):
+    count = pieces[0].shape[0]
+    for k in range(RING):
+        at = pl.multiple_of(axis_place[k] * count, count)
+        held[pl.ds(at, count)] = pieces[k][...]
+
+
+def pair_kernel(place, order, *refs):
+    pieces, (gate_a, gate_b, up_a, up_b) = refs[:RING], refs[RING : RING + 4]
+    outs, held = refs[RING + 4 : -1], refs[-1]
     step = pl.program_id(0)
     half = outs[0].shape[0]
+
+    @pl.when(step == 0)
+    def _():
+        assemble(order, pieces, held)
+
     cols = jnp.concatenate((gate_a[...], gate_b[...], up_a[...], up_b[...]), axis=1)
-    pair = jnp.dot(in_ref[...], cols, preferred_element_type=jnp.float32)
-    lines = jnp.concatenate((down_a[...], down_b[...]), axis=0)
-    back = lax.dot_general(grad_ref[...], lines, LAST, preferred_element_type=jnp.float32)
-    split = pair.shape[1]
+    pair = jnp.dot(held[...], cols, preferred_element_type=jnp.float32)
     for k in range(RING):
 
         @pl.when(step == k)
         def _(k=k):
             for side in range(2):
                 out = outs[2 * k + side]
-                rows = slice(side * half, (side + 1) * half)
-                out[:, :split] = pair[rows].astype(out.dtype)
-                out[:, split:] = back[rows].astype(out.dtype)
-
-
-def partial_terms(place, rows_in, rows_grad, gates, ups, downs):
-    rows, width = rows_in.shape
+                out[...] = pair[side * half : (side + 1) * half].astype(out.dtype)
+
+
+def pair_terms(place, pieces, gates, ups):
+    rows, width = pieces[0].shape[0] * RING, pieces[0].shape[1]
+    half = rows // 2
+    cut = gates[0].shape[1] // RING
+    wide = 2 * cut
+    bf, f32 = jnp.bfloat16, jnp.float32
+    types = (bf, bf, f32, bf, bf, f32, f32, f32)
+    order = (place_of("x") - jnp.arange(RING, dtype=jnp.int32)) % RING
+    cols = pl.BlockSpec((width, cut), lambda step, place, order: (0, place[step]))
+    grid_spec = pltpu.PrefetchScalarGridSpec(
+        num_scalar_prefetch=2,
+        grid=(RING,),
+        in_specs=[pl.BlockSpec(memory_space=pltpu.VMEM)] * RING + [cols] * 4,
+        out_specs=[pl.BlockSpec((half, 2 * wide), lambda *_: (0, 0)) for _ in types],
+        scratch_shapes=[pltpu.VMEM((rows, width), bf)],
+    )
+    return pl.pallas_call(
+        pair_kernel,
+        grid_spec=grid_spec,
+        out_shape=[jax.ShapeDtypeStruct((half, 3 * wide), t) for t in types],
+        cost_estimate=pl.CostEstimate(
+            flops=2 * rows * width * 8 * wide, bytes_accessed=14 << 20, transcendentals=0
+        ),
+        compiler_params=pltpu.CompilerParams(vmem_limit_bytes=VMEM_LIMIT),
+        name="pair",
+    )(place, order, *pieces, *gates, *ups)
+
+
+def hidden_kernel(place, order, *refs):
+    pieces, (down_a, down_b) = refs[:RING], refs[RING : RING + 2]
+    outs, held = refs[RING + 2 + 2 * RING : -1], refs[-1]
+    step = pl.program_id(0)
+    half = outs[0].shape[0]
+    count = half // (2 * RING)
+
+    @pl.when(step == 0)
+    def _():
+        assemble(order, pieces, held)
+
+    lines = jnp.concatenate((down_a[...], down_b[...]), axis=0)
+    back = lax.dot_general(held[...], lines, LAST, preferred_element_type=jnp.float32)
+    for k in range(RING):
+
+        @pl.when(step == k)
+        def _(k=k):
+            for x in range(RING):
+                out = outs[2 * k + x // 2]
+                for z in range(RING):
+                    to, at = ((x % 2) * RING + z) * count, (z * RING + x) * count
+                    out[to : to + count] = back[at : at + count].astype(out.dtype)
+
+
+def hidden_terms(place, pieces, downs, terms):
+    rows, width = pieces[0].shape[0] * RING, pieces[0].shape[1]
     half = rows // 2
     cut = downs[0].shape[0] // RING
     wide = 2 * cut
-    bf, f32 = jnp.bfloat16, jnp.float32
-    types = (bf, bf, f32, bf, bf, f32, f32, f32)
-    act = pl.BlockSpec(memory_space=pltpu.VMEM)
-    cols = pl.BlockSpec((width, cut), lambda step, place: (0, place[step]))
-    lines = pl.BlockSpec((cut, width), lambda step, place: (place[step], 0))
+    order = (place_of("z") - jnp.arange(RING, dtype=jnp.int32)) % RING
+    lines = pl.BlockSpec((cut, width), lambda step, place, order: (place[step], 0))
     grid_spec = pltpu.PrefetchScalarGridSpec(
-        num_scalar_prefetch=1,
+        num_scalar_prefetch=2,
         grid=(RING,),
-        in_specs=[act, act, cols, cols, cols, cols, lines, lines],
-        out_specs=[pl.BlockSpec((half, 3 * wide), lambda step, place: (0, 0)) for _ in types],
-    )
-    return pl.pallas_call(
-        terms_kernel,
+        in_specs=[pl.BlockSpec(memory_space=pltpu.VMEM)] * RING
+        + [lines, lines]
+        + [pl.BlockSpec(memory_space=pl.ANY) for _ in terms],
+        out_specs=[pl.BlockSpec((half, wide), lambda *_: (0, 2)) for _ in terms],
+        scratch_shapes=[pltpu.VMEM((rows, width), jnp.bfloat16)],
+    )
+    return pl.pallas_call(
+        hidden_kernel,
         grid_spec=grid_spec,
-        out_shape=[jax.ShapeDtypeStruct((half, 3 * wide), t) for t in types],
+        out_shape=[jax.ShapeDtypeStruct(t.shape, t.dtype) for t in terms],
+        input_output_aliases={2 + RING + 2 + k: k for k in range(2 * RING)},
         cost_estimate=pl.CostEstimate(
-            flops=2 * rows * width * 12 * wide, bytes_accessed=20 << 20, transcendentals=0
+            flops=2 * rows * width * 4 * wide, bytes_accessed=7 << 20, transcendentals=0
         ),
         compiler_params=pltpu.CompilerParams(vmem_limit_bytes=VMEM_LIMIT),
-        name="terms",
-    )(place, rows_in, rows_grad, *gates, *ups, *downs)
+        name="hidden",
+    )(place, order, *pieces, *downs, *terms)
 
 
 def back_kernel(place, *rest):
@@ -144,16 +227,7 @@
     return narrow(jnp.concatenate((gate_grad, up_grad), axis=1))
 
 
-def first_rows(own_in, own_grad):
-    return gather(own_in, "z", 0), gather(own_grad, "x", 0)
-
-
-def second_rows(some_in, some_grad, width):
-    rows_in = gather(some_in, "x", 0).reshape(-1, width)
-    return rows_in, gather(some_grad, "z", 1).reshape(-1, width)
-
-
-def finish(place, terms, gates, ups, rows):
+def ring_sum(terms):
     far_t, far_b, right_t, right_b, left_t, left_b, own_t, own_b = terms
     far_t = shift(far_t, "y", 1)
     far_b = shift(far_b, "y", -1)
@@ -163,6 +237,11 @@
     left_b = shift(narrow(left_b + far_b), "y", -1)
     top = local_grads(own_t + left_t + right_t)
     low = local_grads(own_b + right_b + left_b)
+    return top, low
+
+
+def finish(place, grads, gates, ups, k):
+    top, low = grads
     from_left_t = shift(top, "y", 1)
     from_right_b = shift(low, "y", -1)
     from_left_b = shift(low, "y", 1)
@@ -171,7 +250,7 @@
     far_low = shift(from_right_b, "y", -1)
     pieces = (far_top, far_low, from_right_t, from_right_b, from_left_t, from_left_b, top, low)
     partial_value = back_terms(place, pieces, gates, ups)
-    blocks = partial_value.reshape(RING * RING, rows, -1)
+    blocks = partial_value.reshape(RING * RING, CHUNKS[k], -1)
     crossed = lax.all_to_all(blocks, XZ, 0, 0)
     return narrow(crossed.astype(jnp.float32).sum(axis=0))
 
@@ -184,27 +263,21 @@
     gates = (gate_weight, swap(gate_weight))
     ups = (up_weight, swap(up_weight))
     downs = (down_weight, swap(down_weight))
-    width = gate_weight.shape[0]
     place = (lax.axis_index("y") + jnp.array(ORDER, jnp.int32)) % RING
+    some_in = join("z", around(inputs, "z"))
+    some_grad = join("x", around(out_grad, "x"))
     results = []
-    at = 0
-    some = terms = None
-    for rows in CHUNKS:
-        own_in = lax.slice_in_dim(inputs, at, at + rows)
-        own_grad = lax.slice_in_dim(out_grad, at, at + rows)
-        at += rows
-        if some is not None:
-            own_in, own_grad, *some = lax.optimization_barrier((own_in, own_grad, *some))
-            filled = second_rows(*some, width)
-            terms = partial_terms(place, *filled, gates, ups, downs)
-        some = first_rows(own_in, own_grad)
+    terms = grads = None
+    for k in range(len(CHUNKS)):
+        in_pieces = around(some_in[k], "x")
+        grad_pieces = around(some_grad[k], "z")
         if terms is not None:
-            *some, terms = lax.optimization_barrier((*some, terms))
-            results.append(finish(place, terms, gates, ups, last))
-        last = rows
-    filled = second_rows(*some, width)
-    terms = partial_terms(place, *filled, gates, ups, downs)
-    results.append(finish(place, terms, gates, ups, rows))
+            sums = ring_sum(terms)
+        if terms is not None:
+            results.append(finish(place, sums, gates, ups, k - 1))
+        terms = pair_terms(place, in_pieces, gates, ups)
+        terms = hidden_terms(place, grad_pieces, downs, terms)
+    results.append(finish(place, ring_sum(terms), gates, ups, k))
     return jnp.concatenate(results, axis=0)
 
 

time: 284 us -> 299 us (1.053)
  the two profiles are of different devices: /device:TPU:0 before, /device:TPU:2 now
where the time goes in v1:
time: 299 us; the launch traced here: 298 us
  waiting for transfers between devices  129 us (43%)
  starting transfers between devices  86.5 us (29%)
  Pallas kernels  54.5 us (18%)
  local copies, waits for them, and re-layouts  17.8 us (6%)
  other arithmetic  10 us (3%)
    ppermute x33, waiting for transfers between devices, shift(): lax.ppermute(value, axis, [(i, (i + step) % RING) for i in range(RING)])  77.7 us
    ppermute x33, starting transfers between devices, shift(): lax.ppermute(value, axis, [(i, (i + step) % RING) for i in range(RING)])  47.3 us
    ppermute x9, starting transfers between devices, shift(): return lax.ppermute(value, ('xl', 'xh'), pairs)  27.9 us
    ppermute x9, waiting for transfers between devices, shift(): return lax.ppermute(value, ('xl', 'xh'), pairs)  27.8 us
    all_to_all x2, waiting for transfers between devices, finish(): crossed = lax.all_to_all(blocks, XZ, 0, 0)  23.8 us
    pallas_call x2, Pallas kernels, pair_terms(): pl.pallas_call(pair_kernel, grid_spec=grid_spec, out_shape=[jax.ShapeDtyp...  20.1 us
    pallas_call x2, Pallas kernels, back_terms(): pl.pallas_call(back_kernel, grid_spec=grid_spec, out_shape=jax.ShapeDtype...  18.6 us
    unnamed x56, local copies, waits for them, and re-layouts  17.8 us
  transfers between devices with their start and end apart: 47, of which 21 were waited for; matrix products, arithmetic and copies ran while one was open for 3% of the time, Pallas kernels for 18%

profile of v1, /device:TPU:2, one launch (start us, length us, event | category | flops | bytes accessed | tf_op | source)
XLA Modules:
  0.0 298.3 jit_solution(5476034599978701761)
XLA Ops:
  8.0 4.0 %collective-permute-done.7.refs_1_ = bf16[80,2048]{1,0:T(8,128)(2,1)S(1)} collective-permute-done((bf16[80,2048]{1,0:T(8,128)(2,1)}, bf16[80,2048]{1,0:T(8,128)(2,1)S(1)}, u32[]{:S(2)}, u32[]{:S(2)}) %collective-permute-start.7) | collective-permute-done | bytes 327712 | tf_op jit(solution)/shard_map/ppermute | solution.py:29
  12.0 8.2 %collective-permute-done.8.refs_2_ = bf16[80,2048]{1,0:T(8,128)(2,1)S(1)} collective-permute-done((bf16[80,2048]{1,0:T(8,128)(2,1)}, bf16[80,2048]{1,0:T(8,128)(2,1)S(1)}, u32[]{:S(2)}, u32[]{:S(2)}) %collective-permute-start.8) | collective-permute-done | bytes 327712 | tf_op jit(solution)/shard_map/ppermute | solution.py:29
  28.2 9.0 %collective-permute-done.1.refs_2_ = bf16[80,2048]{1,0:T(8,128)(2,1)S(1)} collective-permute-done((bf16[80,2048]{1,0:T(8,128)(2,1)}, bf16[80,2048]{1,0:T(8,128)(2,1)S(1)}, u32[]{:S(2)}, u32[]{:S(2)}) %collective-permute-start.1) | collective-permute-done | bytes 327712 | tf_op jit(solution)/shard_map/ppermute | solution.py:28
  44.7 7.5 %collective-permute-start.12 = (bf16[160,2048]{1,0:T(8,128)(2,1)}, bf16[160,2048]{1,0:T(8,128)(2,1)}, u32[]{:S(2)}, u32[]{:S(2)}) collective-permute-start(bf16[160,2048]{1,0:T(8,128)(2,1)} %get-tuple-element.42.refs_0_), channel_id=1, source_target_pairs={{0,66},{64,0},{2,64},{66,2},{1,67},{65,1},{3,65},{67,3},{4,70},{68... | collective-permute-start | bytes 1966088 | tf_op jit(solution)/shard_map/ppermute | solution.py:28
  56.6 4.9 %collective-permute-done.11.refs_2_ = bf16[160,2048]{1,0:T(8,128)(2,1)} collective-permute-done((bf16[160,2048]{1,0:T(8,128)(2,1)}, bf16[160,2048]{1,0:T(8,128)(2,1)}, u32[]{:S(2)}, u32[]{:S(2)}) %collective-permute-start.11) | collective-permute-done | bytes 655392 | tf_op jit(solution)/shard_map/ppermute | solution.py:28
  63.4 10.5 %collective-permute-done.12.refs_3_ = bf16[160,2048]{1,0:T(8,128)(2,1)} collective-permute-done((bf16[160,2048]{1,0:T(8,128)(2,1)}, bf16[160,2048]{1,0:T(8,128)(2,1)}, u32[]{:S(2)}, u32[]{:S(2)}) %collective-permute-start.12) | collective-permute-done | bytes 655392 | tf_op jit(solution)/shard_map/ppermute | solution.py:28
  78.5 13.7 %collective-permute-done.4.refs_2_ = bf16[160,2048]{1,0:T(8,128)(2,1)} collective-permute-done((bf16[160,2048]{1,0:T(8,128)(2,1)S(1)}, bf16[160,2048]{1,0:T(8,128)(2,1)}, u32[]{:S(2)}, u32[]{:S(2)}) %collective-permute-start.4) | collective-permute-done | bytes 655392 | tf_op jit(solution)/shard_map/ppermute | solution.py:29
  92.2 9.0 %collective-permute-start.30 = (bf16[160,2048]{1,0:T(8,128)(2,1)}, bf16[160,2048]{1,0:T(8,128)(2,1)S(1)}, u32[]{:S(2)}, u32[]{:S(2)}) collective-permute-start(bf16[160,2048]{1,0:T(8,128)(2,1)} %copy-done.17), channel_id=1, source_target_pairs={{0,64},{64,2},{2,66},{66,0},{1,65},{65,3},{3,67},{67,1},{4,68},{68... | collective-permute-start | bytes 1966088 | tf_op jit(solution)/shard_map/ppermute | solution.py:28
  107.3 10.1 %pair.2 = (bf16[320,768]{1,0:T(8,128)(2,1)S(1)}, bf16[320,768]{1,0:T(8,128)(2,1)S(1)}, f32[320,768]{1,0:T(8,128)S(1)}, bf16[320,768]{1,0:T(8,128)(2,1)S(1)}, bf1...) custom-call(s32[4]{0:T(128)S(1)} %and_select_fusion.2.place, ...), custom_call_target="tpu_custom_call" | custom-call | flops 5368709120 | bytes 14680064 | tf_op jit(solution)/shard_map/pair/pallas_call | solution.py:105
  118.3 6.3 %hidden.2 = (bf16[320,768]{1,0:T(8,128)(2,1)S(1)}, bf16[320,768]{1,0:T(8,128)(2,1)S(1)}, f32[320,768]{1,0:T(8,128)S(1)}, bf16[320,768]{1,0:T(8,128)(2,1)S(1)}, b...) custom-call(s32[4]{0:T(128)S(1)} %and_select_fusion.2.place, ...), custom_call_target="tpu_custom_call", output_to_operand_aliasing={{0}: (8, {}), {1}: (9, {}), {2}: (10, {}), {3}: (11, {}), {... | custom-call | flops 2684354560 | bytes 7340032 | tf_op jit(solution)/shard_map/hidden/pallas_call | solution.py:157
  137.9 10.0 %pair.3 = (bf16[320,768]{1,0:T(8,128)(2,1)S(1)}, bf16[320,768]{1,0:T(8,128)(2,1)S(1)}, f32[320,768]{1,0:T(8,128)S(1)}, bf16[320,768]{1,0:T(8,128)(2,1)}, bf16[32...) custom-call(s32[4]{0:T(128)S(1)} %and_select_fusion.2.place, ...), custom_call_target="tpu_custom_call" | custom-call | flops 5368709120 | bytes 14680064 | tf_op jit(solution)/shard_map/pair/pallas_call | solution.py:105
  153.2 6.5 %hidden.3 = (bf16[320,768]{1,0:T(8,128)(2,1)S(1)}, bf16[320,768]{1,0:T(8,128)(2,1)S(1)}, f32[320,768]{1,0:T(8,128)S(1)}, bf16[320,768]{1,0:T(8,128)(2,1)}, bf16[...) custom-call(s32[4]{0:T(128)S(1)} %and_select_fusion.2.place, ...), custom_call_target="tpu_custom_call", output_to_operand_aliasing={{0}: (8, {}), {1}: (9, {}), {2}: (10, {}), {3}: (11, {}), {... | custom-call | flops 2684354560 | bytes 7340032 | tf_op jit(solution)/shard_map/hidden/pallas_call | solution.py:157
  162.6 13.0 %collective-permute-done.22 = bf16[320,768]{1,0:T(8,128)(2,1)S(1)} collective-permute-done((bf16[320,768]{1,0:T(8,128)(2,1)S(1)}, bf16[320,768]{1,0:T(8,128)(2,1)S(1)}, u32[]{:S(2)}, u32[]{:S(2)}) %collective-permute-start.22) | collective-permute-done | bytes 491552 | tf_op jit(solution)/shard_map/ppermute | solution.py:29
  181.8 4.3 %collective-permute-done.39 = bf16[320,768]{1,0:T(8,128)(2,1)S(1)} collective-permute-done((bf16[320,768]{1,0:T(8,128)(2,1)S(1)}, bf16[320,768]{1,0:T(8,128)(2,1)S(1)}, u32[]{:S(2)}, u32[]{:S(2)}) %collective-permute-start.39) | collective-permute-done | bytes 491552 | tf_op jit(solution)/shard_map/ppermute | solution.py:29
  189.0 4.2 %collective-permute-done.23.rest_3_ = bf16[320,512]{1,0:T(8,128)(2,1)S(1)} collective-permute-done((bf16[320,512]{1,0:T(8,128)(2,1)S(1)}, bf16[320,512]{1,0:T(8,128)(2,1)S(1)}, u32[]{:S(2)}, u32[]{:S(2)}) %collective-permute-start.23) | collective-permute-done | bytes 327712 | tf_op jit(solution)/shard_map/ppermute | solution.py:29
  197.0 5.7 %collective-permute-done.34 = bf16[320,768]{1,0:T(8,128)(2,1)S(1)} collective-permute-done((bf16[320,768]{1,0:T(8,128)(2,1)S(1)}, bf16[320,768]{1,0:T(8,128)(2,1)S(1)}, u32[]{:S(2)}, u32[]{:S(2)}) %collective-permute-start.34) | collective-permute-done | bytes 491552 | tf_op jit(solution)/shard_map/ppermute | solution.py:29
  203.6 6.1 %collective-permute-done.26.rest_5_ = bf16[320,512]{1,0:T(8,128)(2,1)S(1)} collective-permute-done((bf16[320,512]{1,0:T(8,128)(2,1)S(1)}, bf16[320,512]{1,0:T(8,128)(2,1)S(1)}, u32[]{:S(2)}, u32[]{:S(2)}) %collective-permute-start.26) | collective-permute-done | bytes 327712 | tf_op jit(solution)/shard_map/ppermute | solution.py:29
  211.8 4.9 %collective-permute-done.19.rest_0_ = bf16[320,512]{1,0:T(8,128)(2,1)S(1)} collective-permute-done((bf16[320,512]{1,0:T(8,128)(2,1)S(1)}, bf16[320,512]{1,0:T(8,128)(2,1)S(1)}, u32[]{:S(2)}, u32[]{:S(2)}) %collective-permute-start.19) | collective-permute-done | bytes 327712 | tf_op jit(solution)/shard_map/ppermute | solution.py:29
  216.7 8.9 %back.2 = bf16[640,2048]{1,0:T(8,128)(2,1)S(1)} custom-call(s32[4]{0:T(128)S(1)} %and_select_fusion.2.place, bf16[320,512]{1,0:T(8,128)(2,1)S(1)} %collective-permute-done.19.rest_0_, bf16[320,512]{1,0:T(8,128)(2,1)S(1)} %collective-permute-done.24.rest_1_, bf16[320,512]{1,0:T(8,128)(2,1)S(1)} %collective-permute-done.25.rest_2_, ...), custom_call_target="tpu_custom_call" | custom-call | flops 5368709120 | bytes 14680064 | tf_op jit(solution)/shard_map/back/pallas_call | solution.py:205
  227.2 5.9 %all-to-all-start = ((bf16[16,40,2048]{2,1,0:T(8,128)(2,1)}), bf16[16,40,2048]{2,1,0:T(8,128)(2,1)}, u32[]{:S(2)}, u32[]{:S(2)}) async-start(bf16[16,40,2048]{2,1,0:T(8,128)(2,1)} %bitcast.2), calls=%async_computation | async-start | bytes 5242880 | tf_op jit(solution)/shard_map/all_to_all | solution.py:254
  251.9 4.1 %collective-permute-done.37.rest_0_ = bf16[320,512]{1,0:T(8,128)(2,1)S(1)} collective-permute-done((bf16[320,512]{1,0:T(8,128)(2,1)S(1)}, bf16[320,512]{1,0:T(8,128)(2,1)S(1)}, u32[]{:S(2)}, u32[]{:S(2)}) %collective-permute-start.37) | collective-permute-done | bytes 327712 | tf_op jit(solution)/shard_map/ppermute | solution.py:29
  256.0 9.7 %back.3 = bf16[640,2048]{1,0:T(8,128)(2,1)} custom-call(s32[4]{0:T(128)S(1)} %and_select_fusion.2.place, bf16[320,512]{1,0:T(8,128)(2,1)S(1)} %collective-permute-done.37.rest_0_, bf16[320,512]{1,0:T(8,128)(2,1)S(1)} %collective-permute-done.42.rest_1_, bf16[320,512]{1,0:T(8,128)(2,1)S(1)} %collective-permute-done.43.rest_2_, ...), custom_call_target="tpu_custom_call" | custom-call | flops 5368709120 | bytes 14680064 | tf_op jit(solution)/shard_map/back/pallas_call | solution.py:205
  265.7 5.4 %all-to-all-start.1 = ((bf16[16,40,2048]{2,1,0:T(8,128)(2,1)}), bf16[16,40,2048]{2,1,0:T(8,128)(2,1)S(1)}, u32[]{:S(2)}, u32[]{:S(2)}) async-start(bf16[16,40,2048]{2,1,0:T(8,128)(2,1)} %bitcast.1), calls=%async_computation.1 | async-start | bytes 5242880 | tf_op jit(solution)/shard_map/all_to_all | solution.py:254
  273.3 23.8 %all-to-all-done.1 = bf16[16,40,2048]{2,1,0:T(8,128)(2,1)S(1)} async-done(((bf16[16,40,2048]{2,1,0:T(8,128)(2,1)}), bf16[16,40,2048]{2,1,0:T(8,128)(2,1)S(1)}, u32[]{:S(2)}, u32[]{:S(2)}) %all-to-all-start.1) | async-done | bytes 2621472 | tf_op jit(solution)/shard_map/all_to_all | solution.py:254
  (156 shorter events, 102.3 us)
Async XLA Ops:
  8.0 93.3 %collective-permute-start.13 = (bf16[2048,512]{1,0:T(8,128)(2,1)}, bf16[2048,512]{1,0:T(8,128)(2,1)}, u32[]{:S(2)}, u32[]{:S(2)}) collective-permute-start(bf16[2048,512]{1,0:T(8,128)(2,1)} %rest_8_.3), channel_id=1, source_target_pairs={{0,1},{1,0},{2,3},{3,2},{4,5},{5,4},{6,7},{7,6},{8,9},{9,8},{10,11... | collective-permute-start | bytes 6291464 | tf_op jit(solution)/shard_map/ppermute | solution.py:259
  12.0 92.6 %collective-permute-start.14 = (bf16[2048,512]{1,0:T(8,128)(2,1)}, bf16[2048,512]{1,0:T(8,128)(2,1)}, u32[]{:S(2)}, u32[]{:S(2)}) collective-permute-start(bf16[2048,512]{1,0:T(8,128)(2,1)} %rest_10_.3), channel_id=1, source_target_pairs={{0,1},{1,0},{2,3},{3,2},{4,5},{5,4},{6,7},{7,6},{8,9},{9,8},{10,11... | collective-permute-start | bytes 6291464 | tf_op jit(solution)/shard_map/ppermute | solution.py:259
  38.0 79.5 %collective-permute-start.6 = (bf16[512,2048]{1,0:T(8,128)(2,1)}, bf16[512,2048]{1,0:T(8,128)(2,1)S(1)}, u32[]{:S(2)}, u32[]{:S(2)}) collective-permute-start(bf16[512,2048]{1,0:T(8,128)(2,1)} %refs_4_.7), channel_id=1, source_target_pairs={{0,1},{1,0},{2,3},{3,2},{4,5},{5,4},{6,7},{7,6},{8,9},{9,8},{10,11... | collective-permute-start | bytes 6291464 | tf_op jit(solution)/shard_map/ppermute | solution.py:259
  44.7 29.2 %collective-permute-start.12 = (bf16[160,2048]{1,0:T(8,128)(2,1)}, bf16[160,2048]{1,0:T(8,128)(2,1)}, u32[]{:S(2)}, u32[]{:S(2)}) collective-permute-start(bf16[160,2048]{1,0:T(8,128)(2,1)} %get-tuple-element.42.refs_0_), channel_id=1, source_target_pairs={{0,66},{64,0},{2,64},{66,2},{1,67},{65,1},{3,65},{67,3},{4,70},{68... | collective-permute-start | bytes 1966088 | tf_op jit(solution)/shard_map/ppermute | solution.py:28
  76.6 40.8 %collective-permute-start.5 = (bf16[160,2048]{1,0:T(8,128)(2,1)S(1)}, bf16[160,2048]{1,0:T(8,128)(2,1)S(1)}, u32[]{:S(2)}, u32[]{:S(2)}) collective-permute-start(bf16[160,2048]{1,0:T(8,128)(2,1)S(1)} %get-tuple-element.41.refs_0_), channel_id=1, source_target_pairs={{0,48},{16,0},{32,16},{48,32},{1,49},{17,1},{33,17},{49,33},{2,50}... | collective-permute-start | bytes 1966088 | tf_op jit(solution)/shard_map/ppermute | solution.py:29
  92.2 33.2 %collective-permute-start.30 = (bf16[160,2048]{1,0:T(8,128)(2,1)}, bf16[160,2048]{1,0:T(8,128)(2,1)S(1)}, u32[]{:S(2)}, u32[]{:S(2)}) collective-permute-start(bf16[160,2048]{1,0:T(8,128)(2,1)} %copy-done.17), channel_id=1, source_target_pairs={{0,64},{64,2},{2,66},{66,0},{1,65},{65,3},{3,67},{67,1},{4,68},{68... | collective-permute-start | bytes 1966088 | tf_op jit(solution)/shard_map/ppermute | solution.py:28
  101.3 27.5 %collective-permute-start.31 = (bf16[160,2048]{1,0:T(8,128)(2,1)}, bf16[160,2048]{1,0:T(8,128)(2,1)S(1)}, u32[]{:S(2)}, u32[]{:S(2)}) collective-permute-start(bf16[160,2048]{1,0:T(8,128)(2,1)} %copy-done.17), channel_id=1, source_target_pairs={{0,2},{64,66},{2,0},{66,64},{1,3},{65,67},{3,1},{67,65},{4,6},{68,... | collective-permute-start | bytes 1966088 | tf_op jit(solution)/shard_map/ppermute | solution.py:28
  104.6 28.0 %collective-permute-start.32 = (bf16[160,2048]{1,0:T(8,128)(2,1)}, bf16[160,2048]{1,0:T(8,128)(2,1)S(1)}, u32[]{:S(2)}, u32[]{:S(2)}) collective-permute-start(bf16[160,2048]{1,0:T(8,128)(2,1)} %copy-done.17), channel_id=1, source_target_pairs={{0,66},{64,0},{2,64},{66,2},{1,67},{65,1},{3,65},{67,3},{4,70},{68... | collective-permute-start | bytes 1966088 | tf_op jit(solution)/shard_map/ppermute | solution.py:28
  117.4 33.3 %collective-permute-start.27 = (bf16[160,2048]{1,0:T(8,128)(2,1)}, bf16[160,2048]{1,0:T(8,128)(2,1)S(1)}, u32[]{:S(2)}, u32[]{:S(2)}) collective-permute-start(bf16[160,2048]{1,0:T(8,128)(2,1)} %get-tuple-element.59.refs_0_), channel_id=1, source_target_pairs={{0,16},{16,32},{32,48},{48,0},{1,17},{17,33},{33,49},{49,1},{2,18}... | collective-permute-start | bytes 1966088 | tf_op jit(solution)/shard_map/ppermute | solution.py:29
  117.5 35.0 %collective-permute-start.28 = (bf16[160,2048]{1,0:T(8,128)(2,1)}, bf16[160,2048]{1,0:T(8,128)(2,1)S(1)}, u32[]{:S(2)}, u32[]{:S(2)}) collective-permute-start(bf16[160,2048]{1,0:T(8,128)(2,1)} %get-tuple-element.59.refs_0_), channel_id=1, source_target_pairs={{0,32},{16,48},{32,0},{48,16},{1,33},{17,49},{33,1},{49,17},{2,34}... | collective-permute-start | bytes 1966088 | tf_op jit(solution)/shard_map/ppermute | solution.py:29
  126.2 27.0 %collective-permute-start.29 = (bf16[160,2048]{1,0:T(8,128)(2,1)}, bf16[160,2048]{1,0:T(8,128)(2,1)S(1)}, u32[]{:S(2)}, u32[]{:S(2)}) collective-permute-start(bf16[160,2048]{1,0:T(8,128)(2,1)} %get-tuple-element.59.refs_0_), channel_id=1, source_target_pairs={{0,48},{16,0},{32,16},{48,32},{1,49},{17,1},{33,17},{49,33},{2,50}... | collective-permute-start | bytes 1966088 | tf_op jit(solution)/shard_map/ppermute | solution.py:29
  133.5 29.1 %collective-permute-start.20 = (bf16[320,768]{1,0:T(8,128)(2,1)S(1)}, bf16[320,768]{1,0:T(8,128)(2,1)}, u32[]{:S(2)}, u32[]{:S(2)}) collective-permute-start(bf16[320,768]{1,0:T(8,128)(2,1)S(1)} %get-tuple-element.56), channel_id=1, source_target_pairs={{0,4},{4,8},{8,12},{12,0},{1,5},{5,9},{9,13},{13,1},{2,6},{6,10},{... | collective-permute-start | bytes 1474568 | tf_op jit(solution)/shard_map/ppermute | solution.py:29
  150.7 29.2 %collective-permute-start.15 = (bf16[320,768]{1,0:T(8,128)(2,1)}, bf16[320,768]{1,0:T(8,128)(2,1)S(1)}, u32[]{:S(2)}, u32[]{:S(2)}) collective-permute-start(bf16[320,768]{1,0:T(8,128)(2,1)} %copy-done.4), channel_id=1, source_target_pairs={{0,12},{4,0},{8,4},{12,8},{1,13},{5,1},{9,5},{13,9},{2,14},{6,2},{... | collective-permute-start | bytes 1474568 | tf_op jit(solution)/shard_map/ppermute | solution.py:29
  152.4 23.2 %collective-permute-start.22 = (bf16[320,768]{1,0:T(8,128)(2,1)S(1)}, bf16[320,768]{1,0:T(8,128)(2,1)S(1)}, u32[]{:S(2)}, u32[]{:S(2)}) collective-permute-start(bf16[320,768]{1,0:T(8,128)(2,1)S(1)} %add_convert_fusion.2), channel_id=1, source_target_pairs={{0,12},{4,0},{8,4},{12,8},{1,13},{5,1},{9,5},{13,9},{2,14},{6,2},{... | collective-permute-start | bytes 1474568 | tf_op jit(solution)/shard_map/ppermute | solution.py:29
  159.8 26.4 %collective-permute-start.39 = (bf16[320,768]{1,0:T(8,128)(2,1)S(1)}, bf16[320,768]{1,0:T(8,128)(2,1)S(1)}, u32[]{:S(2)}, u32[]{:S(2)}) collective-permute-start(bf16[320,768]{1,0:T(8,128)(2,1)S(1)} %get-tuple-element.76), channel_id=1, source_target_pairs={{0,12},{4,0},{8,4},{12,8},{1,13},{5,1},{9,5},{13,9},{2,14},{6,2},{... | collective-permute-start | bytes 1474568 | tf_op jit(solution)/shard_map/ppermute | solution.py:29
  180.4 22.3 %collective-permute-start.34 = (bf16[320,768]{1,0:T(8,128)(2,1)S(1)}, bf16[320,768]{1,0:T(8,128)(2,1)S(1)}, u32[]{:S(2)}, u32[]{:S(2)}) collective-permute-start(bf16[320,768]{1,0:T(8,128)(2,1)S(1)} %get-tuple-element.72), channel_id=1, source_target_pairs={{0,4},{4,8},{8,12},{12,0},{1,5},{5,9},{9,13},{13,1},{2,6},{6,10},{... | collective-permute-start | bytes 1474568 | tf_op jit(solution)/shard_map/ppermute | solution.py:29
  180.8 28.9 %collective-permute-start.26 = (bf16[320,512]{1,0:T(8,128)(2,1)S(1)}, bf16[320,512]{1,0:T(8,128)(2,1)S(1)}, u32[]{:S(2)}, u32[]{:S(2)}) collective-permute-start(bf16[320,512]{1,0:T(8,128)(2,1)S(1)} %pad_maximum_fusion.1.rest_7_), channel_id=1, source_target_pairs={{0,4},{4,8},{8,12},{12,0},{1,5},{5,9},{9,13},{13,1},{2,6},{6,10},{... | collective-permute-start | bytes 983048 | tf_op jit(solution)/shard_map/ppermute | solution.py:29
  186.1 23.6 %collective-permute-start.25 = (bf16[320,512]{1,0:T(8,128)(2,1)S(1)}, bf16[320,512]{1,0:T(8,128)(2,1)S(1)}, u32[]{:S(2)}, u32[]{:S(2)}) collective-permute-start(bf16[320,512]{1,0:T(8,128)(2,1)S(1)} %pad_maximum_fusion.rest_6_), channel_id=1, source_target_pairs={{0,12},{4,0},{8,4},{12,8},{1,13},{5,1},{9,5},{13,9},{2,14},{6,2},{... | collective-permute-start | bytes 983048 | tf_op jit(solution)/shard_map/ppermute | solution.py:29
  202.7 30.4 %collective-permute-start.38 = (bf16[320,768]{1,0:T(8,128)(2,1)}, bf16[320,768]{1,0:T(8,128)(2,1)S(1)}, u32[]{:S(2)}, u32[]{:S(2)}) collective-permute-start(bf16[320,768]{1,0:T(8,128)(2,1)} %get-tuple-element.74), channel_id=1, source_target_pairs={{0,4},{4,8},{8,12},{12,0},{1,5},{5,9},{9,13},{13,1},{2,6},{6,10},{... | collective-permute-start | bytes 1474568 | tf_op jit(solution)/shard_map/ppermute | solution.py:29
  209.7 25.7 %collective-permute-start.33 = (bf16[320,768]{1,0:T(8,128)(2,1)}, bf16[320,768]{1,0:T(8,128)(2,1)S(1)}, u32[]{:S(2)}, u32[]{:S(2)}) collective-permute-start(bf16[320,768]{1,0:T(8,128)(2,1)} %get-tuple-element.70), channel_id=1, source_target_pairs={{0,12},{4,0},{8,4},{12,8},{1,13},{5,1},{9,5},{13,9},{2,14},{6,2},{... | collective-permute-start | bytes 1474568 | tf_op jit(solution)/shard_map/ppermute | solution.py:29
  209.7 23.4 %collective-permute-start.40 = (bf16[320,768]{1,0:T(8,128)(2,1)}, bf16[320,768]{1,0:T(8,128)(2,1)}, u32[]{:S(2)}, u32[]{:S(2)}) collective-permute-start(bf16[320,768]{1,0:T(8,128)(2,1)} %add_convert_fusion), channel_id=1, source_target_pairs={{0,12},{4,0},{8,4},{12,8},{1,13},{5,1},{9,5},{13,9},{2,14},{6,2},{... | collective-permute-start | bytes 1474568 | tf_op jit(solution)/shard_map/ppermute | solution.py:29
  209.7 25.7 %collective-permute-start.35 = (bf16[320,768]{1,0:T(8,128)(2,1)}, bf16[320,768]{1,0:T(8,128)(2,1)S(1)}, u32[]{:S(2)}, u32[]{:S(2)}) collective-permute-start(bf16[320,768]{1,0:T(8,128)(2,1)} %add_convert_fusion.1), channel_id=1, source_target_pairs={{0,4},{4,8},{8,12},{12,0},{1,5},{5,9},{9,13},{13,1},{2,6},{6,10},{... | collective-permute-start | bytes 1474568 | tf_op jit(solution)/shard_map/ppermute | solution.py:29
  227.2 38.5 %all-to-all-start = ((bf16[16,40,2048]{2,1,0:T(8,128)(2,1)}), bf16[16,40,2048]{2,1,0:T(8,128)(2,1)}, u32[]{:S(2)}, u32[]{:S(2)}) async-start(bf16[16,40,2048]{2,1,0:T(8,128)(2,1)} %bitcast.2), calls=%async_computation | async-start | bytes 5242880 | tf_op jit(solution)/shard_map/all_to_all | solution.py:254
  265.7 31.4 %all-to-all-start.1 = ((bf16[16,40,2048]{2,1,0:T(8,128)(2,1)}), bf16[16,40,2048]{2,1,0:T(8,128)(2,1)S(1)}, u32[]{:S(2)}, u32[]{:S(2)}) async-start(bf16[16,40,2048]{2,1,0:T(8,128)(2,1)} %bitcast.1), calls=%async_computation.1 | async-start | bytes 5242880 | tf_op jit(solution)/shard_map/all_to_all | solution.py:254
  (51 other events, 642.6 us)

commit v2 on v1

v2 whole, which is shorter than its diff:
```python
import functools

import jax
import jax.numpy as jnp
from jax import lax
from jax.experimental import pallas as pl
from jax.experimental.pallas import tpu as pltpu
from jax.sharding import Mesh, PartitionSpec as P

CHUNKS = (40, 40)
RING = 4
XZ = ("xh", "xl", "z")
ORDER = (2, 1, 3, 0)
STEPS = (0, 1, 3, 2)
LAST = (((1,), (1,)), ((), ()))
VMEM_LIMIT = 46 << 20


def place_of(axis):
    if axis == "x":
        return lax.axis_index("xh") * 2 + lax.axis_index("xl")
    return lax.axis_index(axis)


def shift(value, axis, step):
    if axis == "x":
        order = lambda i: (i % 2) * 2 + i // 2
        pairs = [(order(i), order((i + step) % RING)) for i in range(RING)]
        return lax.ppermute(value, ("xl", "xh"), pairs)
    return lax.ppermute(value, axis, [(i, (i + step) % RING) for i in range(RING)])


def around(value, axis):
    return [value] + [shift(value, axis, step) for step in STEPS[1:]]


def join_kernel(rows, *refs):
    pieces, outs = refs[:RING], refs[RING:]
    for k in range(RING):
        at = 0
        for count, out in zip(rows, outs):
            out[k * count : (k + 1) * count] = pieces[k][at : at + count]
            at += count


def join(pieces):
    width = pieces[0].shape[1]
    spec = pl.BlockSpec(memory_space=pltpu.VMEM)
    return pl.pallas_call(
        functools.partial(join_kernel, CHUNKS),
        in_specs=[spec] * RING,
        out_specs=[spec] * len(CHUNKS),
        out_shape=[jax.ShapeDtypeStruct((RING * rows, width), pieces[0].dtype) for rows in CHUNKS],
        cost_estimate=pl.CostEstimate(flops=1 << 20, bytes_accessed=3 << 20, transcendentals=0),
        compiler_params=pltpu.CompilerParams(vmem_limit_bytes=16 << 20),
        name="join",
    )(*pieces)


def assemble(pieces, held):
    count = pieces[0].shape[0]
    for k, piece in enumerate(pieces):
        held[k * count : (k + 1) * count] = piece[...]


def pair_kernel(place, *refs, count, sides):
    pieces, (gate_a, gate_b, up_a, up_b) = refs[:count], refs[count : count + 4]
    outs, held = refs[-1 - RING * len(sides) : -1], refs[-1]
    step = pl.program_id(0)

    @pl.when(step == 0)
    def _():
        assemble(pieces, held)

    cols = jnp.concatenate((gate_a[...], gate_b[...], up_a[...], up_b[...]), axis=1)
    pair = jnp.dot(held[...], cols, preferred_element_type=jnp.float32)
    for k in range(RING):

        @pl.when(step == k)
        def _(k=k):
            at = 0
            for n in range(len(sides)):
                out = outs[len(sides) * k + n]
                out[...] = pair[at : at + out.shape[0]].astype(out.dtype)
                at += out.shape[0]


def pair_terms(place, pieces, gates, ups, first, terms):
    block, width = pieces[0].shape
    count = len(pieces)
    cut = gates[0].shape[1] // RING
    wide = 2 * cut
    bf, f32 = jnp.bfloat16, jnp.float32
    types = (bf, bf, f32, bf, bf, f32, f32, f32)
    sides, specs = [], []
    for side in range(2):
        low, high = max(first, 2 * side), min(first + count, 2 * side + 2)
        if low < high:
            sides.append(side)
            index = (low - 2 * side) // (high - low)
            specs.append(pl.BlockSpec(((high - low) * block, 2 * wide), lambda *_, i=index: (i, 0)))
    touched = [2 * k + side for k in range(RING) for side in sides]
    old = [] if terms is None else [terms[k] for k in touched]
    cols = pl.BlockSpec((width, cut), lambda step, place: (0, place[step]))
    grid_spec = pltpu.PrefetchScalarGridSpec(
        num_scalar_prefetch=1,
        grid=(RING,),
        in_specs=[pl.BlockSpec(memory_space=pltpu.VMEM)] * count
        + [cols] * 4
        + [pl.BlockSpec(memory_space=pl.ANY) for _ in old],
        out_specs=specs * RING,
        scratch_shapes=[pltpu.VMEM((count * block, width), bf)],
    )
    new = pl.pallas_call(
        functools.partial(pair_kernel, count=count, sides=tuple(sides)),
        grid_spec=grid_spec,
        out_shape=[jax.ShapeDtypeStruct((2 * block, 3 * wide), types[k]) for k in touched],
        input_output_aliases={1 + count + 4 + k: k for k in range(len(old))},
        cost_estimate=pl.CostEstimate(
            flops=2 * count * block * width * 8 * wide, bytes_accessed=14 << 20, transcendentals=0
        ),
        compiler_params=pltpu.CompilerParams(vmem_limit_bytes=VMEM_LIMIT),
        name="pair",
    )(place, *pieces, *gates, *ups, *old)
    if terms is None:
        return new
    terms = list(terms)
    for k, value in zip(touched, new):
        terms[k] = value
    return terms


def hidden_kernel(place, *refs):
    pieces, (down_a, down_b) = refs[:RING], refs[RING : RING + 2]
    refs, held = refs[RING + 2 : -1], refs[-1]
    outs = refs[len(refs) // 2 :]
    step = pl.program_id(0)
    half = outs[0].shape[0]
    count = half // (2 * RING)

    @pl.when(step == 0)
    def _():
        assemble(pieces, held)

    lines = jnp.concatenate((down_a[...], down_b[...]), axis=0)
    back = lax.dot_general(held[...], lines, LAST, preferred_element_type=jnp.float32)
    for k in range(len(outs) // 2):

        @pl.when(step == k)
        def _(k=k):
            for x in range(RING):
                out = outs[2 * k + x // 2]
                for z in range(RING):
                    to, at = ((x % 2) * RING + z) * count, (z * RING + x) * count
                    out[to : to + count] = back[at : at + count].astype(out.dtype)


def hidden_terms(place, pieces, downs, terms, first):
    rows, width = pieces[0].shape[0] * RING, pieces[0].shape[1]
    half = rows // 2
    steps = len(terms) // 2
    cut = downs[0].shape[0] // RING
    wide = 2 * cut
    lines = pl.BlockSpec((cut, width), lambda step, place: (place[step + first], 0))
    grid_spec = pltpu.PrefetchScalarGridSpec(
        num_scalar_prefetch=1,
        grid=(steps,),
        in_specs=[pl.BlockSpec(memory_space=pltpu.VMEM)] * RING
        + [lines, lines]
        + [pl.BlockSpec(memory_space=pl.ANY) for _ in terms],
        out_specs=[pl.BlockSpec((half, wide), lambda *_: (0, 2)) for _ in terms],
        scratch_shapes=[pltpu.VMEM((rows, width), jnp.bfloat16)],
    )
    return pl.pallas_call(
        hidden_kernel,
        grid_spec=grid_spec,
        out_shape=[jax.ShapeDtypeStruct(t.shape, t.dtype) for t in terms],
        input_output_aliases={1 + RING + 2 + k: k for k in range(2 * steps)},
        cost_estimate=pl.CostEstimate(
            flops=2 * rows * width * steps * wide, bytes_accessed=7 << 20, transcendentals=0
        ),
        compiler_params=pltpu.CompilerParams(vmem_limit_bytes=VMEM_LIMIT),
        name="hidden",
    )(place, *pieces, *downs, *terms)


def back_kernel(place, target, *rest):
    pieces, cols, out_ref, held = rest[:8], rest[8:12], rest[12], rest[13]
    half = pieces[0].shape[0]
    cut = pieces[0].shape[1] // 4
    span = RING * cut

    @pl.when(pl.program_id(0) == 0)
    def _():
        for k in range(RING):
            at = pl.multiple_of(place[k] * cut, cut)
            for side in range(2):
                for part in range(4):
                    held[side * half : (side + 1) * half, pl.ds(at + part * span, cut)] = pieces[
                        2 * k + side
                    ][:, part * cut : (part + 1) * cut]

    total = lax.dot_general(
        held[...],
        jnp.concatenate([c[...] for c in cols], axis=1),
        LAST,
        preferred_element_type=jnp.float32,
    )
    count = out_ref.shape[1]
    for k in range(RING * RING):
        out_ref[target[k]] = total[k * count : (k + 1) * count].astype(out_ref.dtype)


def back_terms(place, pieces, gates, ups, rows_cut=512):
    half = pieces[0].shape[0]
    width, span = gates[0].shape
    count = 2 * half // (RING * RING)
    steps = jnp.array(STEPS, jnp.int32)
    x = (place_of("x") - steps) % RING
    z = (place_of("z") - steps) % RING
    target = (x[:, None] * RING + z[None, :]).reshape(-1)
    grid_spec = pltpu.PrefetchScalarGridSpec(
        num_scalar_prefetch=2,
        grid=(width // rows_cut,),
        in_specs=[pl.BlockSpec(memory_space=pltpu.VMEM) for _ in pieces]
        + [pl.BlockSpec((rows_cut, span), lambda n, *_: (n, 0)) for _ in range(4)],
        out_specs=pl.BlockSpec((RING * RING, count, rows_cut), lambda n, *_: (0, 0, n)),
        scratch_shapes=[pltpu.VMEM((2 * half, 4 * span), jnp.bfloat16)],
    )
    return pl.pallas_call(
        back_kernel,
        grid_spec=grid_spec,
        out_shape=jax.ShapeDtypeStruct((RING * RING, count, width), jnp.bfloat16),
        cost_estimate=pl.CostEstimate(
            flops=16 * half * width * span, bytes_accessed=14 << 20, transcendentals=0
        ),
        compiler_params=pltpu.CompilerParams(vmem_limit_bytes=VMEM_LIMIT),
        name="back",
    )(place, target, *pieces, *gates, *ups)


def narrow(value):
    return value.astype(jnp.bfloat16)


def local_grads(total):
    wide = total.shape[1] // 3
    gate, upper, hidden_grad = total[:, :wide], total[:, wide : 2 * wide], total[:, 2 * wide :]
    logistic = jax.nn.sigmoid(gate)
    gate_grad = hidden_grad * upper * logistic * (1.0 + gate * (1.0 - logistic))
    up_grad = hidden_grad * gate * logistic
    return narrow(jnp.concatenate((gate_grad, up_grad), axis=1))


def ring_sum(terms):
    far_t, far_b, right_t, right_b, left_t, left_b, own_t, own_b = terms
    far_t = shift(far_t, "y", 1)
    far_b = shift(far_b, "y", -1)
    right_b = shift(right_b, "y", 1)
    left_t = shift(left_t, "y", -1)
    right_t = shift(narrow(right_t + far_t), "y", 1)
    left_b = shift(narrow(left_b + far_b), "y", -1)
    top = local_grads(own_t + left_t + right_t)
    low = local_grads(own_b + right_b + left_b)
    return top, low


def finish(place, grads, gates, ups):
    top, low = grads
    from_left_t = shift(top, "y", 1)
    from_right_b = shift(low, "y", -1)
    from_left_b = shift(low, "y", 1)
    from_right_t = shift(top, "y", -1)
    far_top = shift(from_left_t, "y", 1)
    far_low = shift(from_right_b, "y", -1)
    pieces = (far_top, far_low, from_right_t, from_right_b, from_left_t, from_left_b, top, low)
    partial_value = back_terms(place, pieces, gates, ups)
    crossed = lax.all_to_all(partial_value, XZ, 0, 0)
    return narrow(crossed.astype(jnp.float32).sum(axis=0))


def swap(value):
    return lax.ppermute(value, "core", [(0, 1), (1, 0)])


def step_shards(inputs, out_grad, gate_weight, up_weight, down_weight):
    gates = (gate_weight, swap(gate_weight))
    ups = (up_weight, swap(up_weight))
    downs = (down_weight, swap(down_weight))
    place = (lax.axis_index("y") + jnp.array(ORDER, jnp.int32)) % RING
    some_in = join(around(inputs, "z"))
    some_grad = join(around(out_grad, "x"))
    results = []
    terms = grads = None
    for k in range(len(CHUNKS)):
        in_pieces = around(some_in[k], "x")
        grad_pieces = around(some_grad[k], "z")
        if terms is not None:
            sums = ring_sum(terms)
        if terms is not None:
            results.append(finish(place, sums, gates, ups))
        if k:
            terms = pair_terms(place, in_pieces, gates, ups, 0, None)
        else:
            terms = pair_terms(place, in_pieces[:3], gates, ups, 0, None)
            terms = pair_terms(place, in_pieces[3:], gates, ups, 3, terms)
        far = hidden_terms(place, grad_pieces, downs, terms[:2], 0)
        near = hidden_terms(place, grad_pieces, downs, terms[2:], 1)
        terms = [*far, *near]
    results.append(finish(place, ring_sum(terms), gates, ups))
    return jnp.concatenate(results, axis=0)


def solution(mesh):
    fine = Mesh(mesh.devices.reshape(2, 4, 4, 2, 2), ("xl", "z", "y", "xh", "core"))
    tokens = ("xl", "z", "xh", "core")
    return jax.shard_map(
        step_shards,
        mesh=fine,
        in_specs=(P(tokens, "y"), P(tokens, "y"), P("y", tokens), P("y", tokens), P(tokens, "y")),
        out_specs=P(tokens, "y"),
        check_vma=False,
    )
```

time: 299 us -> 283 us (0.946)
  the two profiles are of different devices: /device:TPU:2 before, /device:TPU:0 now
where the time goes in v2:
time: 283 us; the launch traced here: 282 us
  waiting for transfers between devices  94.9 us (34%)
  starting transfers between devices  81.2 us (29%)
  Pallas kernels  65.1 us (23%)
  local copies, waits for them, and re-layouts  25.9 us (9%)
  other arithmetic  14 us (5%)
    ppermute x33, starting transfers between devices, shift(): lax.ppermute(value, axis, [(i, (i + step) % RING) for i in range(RING)])  51.5 us
    ppermute x33, waiting for transfers between devices, shift(): lax.ppermute(value, axis, [(i, (i + step) % RING) for i in range(RING)])  51.3 us
    pallas_call x3, Pallas kernels, pair_terms(): pl.pallas_call(functools.partial(pair_kernel, count=count, sides=tuple(si...  26.3 us
    unnamed x102, local copies, waits for them, and re-layouts  25.8 us
    ppermute x9, waiting for transfers between devices, shift(): return lax.ppermute(value, ('xl', 'xh'), pairs)  23.8 us
    pallas_call x2, Pallas kernels, back_terms(): pl.pallas_call(back_kernel, grid_spec=grid_spec, out_shape=jax.ShapeDtype...  20.3 us
    all_to_all x2, waiting for transfers between devices, finish(): crossed = lax.all_to_all(partial_value, XZ, 0, 0)  19.8 us
    ppermute x9, starting transfers between devices, shift(): return lax.ppermute(value, ('xl', 'xh'), pairs)  18.6 us
  transfers between devices with their start and end apart: 47, of which 13 were waited for; matrix products, arithmetic and copies ran while one was open for 5% of the time, Pallas kernels for 23%

profile of v2, /device:TPU:0, one launch (start us, length us, event | category | flops | bytes accessed | tf_op | source)
XLA Modules:
  0.0 281.5 jit_solution(6718399533328093843)
XLA Ops:
  4.7 8.2 %collective-permute-done.7.refs_1_ = bf16[80,2048]{1,0:T(8,128)(2,1)S(1)} collective-permute-done((bf16[80,2048]{1,0:T(8,128)(2,1)}, bf16[80,2048]{1,0:T(8,128)(2,1)S(1)}, u32[]{:S(2)}, u32[]{:S(2)}) %collective-permute-start.7) | collective-permute-done | bytes 327712 | tf_op jit(solution)/shard_map/ppermute | solution.py:30
  15.9 7.8 %collective-permute-done.9.refs_3_ = bf16[80,2048]{1,0:T(8,128)(2,1)S(1)} collective-permute-done((bf16[80,2048]{1,0:T(8,128)(2,1)}, bf16[80,2048]{1,0:T(8,128)(2,1)S(1)}, u32[]{:S(2)}, u32[]{:S(2)}) %collective-permute-start.9) | collective-permute-done | bytes 327712 | tf_op jit(solution)/shard_map/ppermute | solution.py:30
  29.4 10.2 %collective-permute-done.1.refs_2_ = bf16[80,2048]{1,0:T(8,128)(2,1)S(1)} collective-permute-done((bf16[80,2048]{1,0:T(8,128)(2,1)}, bf16[80,2048]{1,0:T(8,128)(2,1)S(1)}, u32[]{:S(2)}, u32[]{:S(2)}) %collective-permute-start.1) | collective-permute-done | bytes 327712 | tf_op jit(solution)/shard_map/ppermute | solution.py:29
  39.6 3.6 %collective-permute-start.11 = (bf16[160,2048]{1,0:T(8,128)(2,1)}, bf16[160,2048]{1,0:T(8,128)(2,1)S(1)}, u32[]{:S(2)}, u32[]{:S(2)}) collective-permute-start(bf16[160,2048]{1,0:T(8,128)(2,1)} %get-tuple-element.46.refs_0_), channel_id=1, source_target_pairs={{0,66},{64,0},{2,64},{66,2},{1,67},{65,1},{3,65},{67,3},{4,70},{68... | collective-permute-start | bytes 1966088 | tf_op jit(solution)/shard_map/ppermute | solution.py:29
  43.1 12.0 %collective-permute-done.10.refs_1_ = bf16[160,2048]{1,0:T(8,128)(2,1)S(1)} collective-permute-done((bf16[160,2048]{1,0:T(8,128)(2,1)}, bf16[160,2048]{1,0:T(8,128)(2,1)S(1)}, u32[]{:S(2)}, u32[]{:S(2)}) %collective-permute-start.10) | collective-permute-done | bytes 655392 | tf_op jit(solution)/shard_map/ppermute | solution.py:29
  62.0 5.8 %collective-permute-start.3 = (bf16[160,2048]{1,0:T(8,128)(2,1)S(1)}, bf16[160,2048]{1,0:T(8,128)(2,1)S(1)}, u32[]{:S(2)}, u32[]{:S(2)}) collective-permute-start(bf16[160,2048]{1,0:T(8,128)(2,1)S(1)} %get-tuple-element.45.refs_0_), channel_id=1, source_target_pairs={{0,16},{16,32},{32,48},{48,0},{1,17},{17,33},{33,49},{49,1},{2,18}... | collective-permute-start | bytes 1966088 | tf_op jit(solution)/shard_map/ppermute | solution.py:30
  72.1 9.0 %pair.3 = (bf16[320,768]{1,0:T(8,128)(2,1)S(1)}, bf16[320,768]{1,0:T(8,128)(2,1)S(1)}, f32[320,768]{1,0:T(8,128)S(1)}, bf16[320,768]{1,0:T(8,128)(2,1)}, bf16[32...) custom-call(s32[4]{0:T(128)S(1)} %and_select_fusion.2.place, ...), custom_call_target="tpu_custom_call" | custom-call | flops 4026531840 | bytes 14680064 | tf_op jit(solution)/shard_map/pair/pallas_call | solution.py:114
  83.9 4.4 %collective-permute-start.30 = (bf16[160,2048]{1,0:T(8,128)(2,1)}, bf16[160,2048]{1,0:T(8,128)(2,1)}, u32[]{:S(2)}, u32[]{:S(2)}) collective-permute-start(bf16[160,2048]{1,0:T(8,128)(2,1)} %get-tuple-element.68.refs_0_), channel_id=1, source_target_pairs={{0,64},{64,2},{2,66},{66,0},{1,65},{65,3},{3,67},{67,1},{4,68},{68... | collective-permute-start | bytes 1966088 | tf_op jit(solution)/shard_map/ppermute | solution.py:29
  88.3 6.5 %pair.4 = (bf16[320,768]{1,0:T(8,128)(2,1)S(1)}, bf16[320,768]{1,0:T(8,128)(2,1)}, f32[320,768]{1,0:T(8,128)S(1)}, f32[320,768]{1,0:T(8,128)S(1)}) custom-call(s32[4]{0:T(128)S(1)} %and_select_fusion.2.place, bf16[160,2048]{1,0:T(8,128)(2,1)} %collective-permute-done.14.refs_0_, ...), custom_call_target="tpu_custom_call", output_to_operand_aliasing={{0}: (6, {}), {1}: (7, {}), {2}: (8, {}), {3}: (9, {})} | custom-call | flops 1342177280 | bytes 14680064 | tf_op jit(solution)/shard_map/pair/pallas_call | solution.py:114
  112.1 5.7 %hidden.4 = (f32[320,768]{1,0:T(8,128)S(1)}, bf16[320,768]{1,0:T(8,128)(2,1)}, bf16[320,768]{1,0:T(8,128)(2,1)S(1)}, f32[320,768]{1,0:T(8,128)S(1)}, f32[320,768]{1,0:T(8,128)S(1)}, /*index=5*/f32[320,768]{1,0:T(8,128)S(1)}) custom-call(s32[4]{0:T(128)S(1)} %and_select_fusion.2.place, ...), custom_call_target="tpu_custom_call", output_to_operand_aliasing={{0}: (7, {}), {1}: (8, {}), {2}: (9, {}), {3}: (10, {}), {4... | custom-call | flops 2013265920 | bytes 7340032 | tf_op jit(solution)/shard_map/hidden/pallas_call | solution.py:174
  128.8 10.8 %pair.5 = (bf16[320,768]{1,0:T(8,128)(2,1)}, bf16[320,768]{1,0:T(8,128)(2,1)}, f32[320,768]{1,0:T(8,128)S(1)}, bf16[320,768]{1,0:T(8,128)(2,1)S(1)}, bf16[320,76...) custom-call(s32[4]{0:T(128)S(1)} %and_select_fusion.2.place, ...), custom_call_target="tpu_custom_call" | custom-call | flops 5368709120 | bytes 14680064 | tf_op jit(solution)/shard_map/pair/pallas_call | solution.py:114
  146.6 4.7 %collective-permute-done.16 = bf16[320,768]{1,0:T(8,128)(2,1)S(1)} collective-permute-done((bf16[320,768]{1,0:T(8,128)(2,1)S(1)}, bf16[320,768]{1,0:T(8,128)(2,1)S(1)}, u32[]{:S(2)}, u32[]{:S(2)}) %collective-permute-start.16) | collective-permute-done | bytes 491552 | tf_op jit(solution)/shard_map/ppermute | solution.py:30
  152.6 3.2 %collective-permute-start.23 = (bf16[320,512]{1,0:T(8,128)(2,1)}, bf16[320,512]{1,0:T(8,128)(2,1)}, u32[]{:S(2)}, u32[]{:S(2)}) collective-permute-start(bf16[320,512]{1,0:T(8,128)(2,1)} %pad_maximum_fusion.1.rest_7_), channel_id=1, source_target_pairs={{0,12},{4,0},{8,4},{12,8},{1,13},{5,1},{9,5},{13,9},{2,14},{6,2},{... | collective-permute-start | bytes 983048 | tf_op jit(solution)/shard_map/ppermute | solution.py:30
  155.8 16.5 %collective-permute-done.17 = bf16[320,768]{1,0:T(8,128)(2,1)S(1)} collective-permute-done((bf16[320,768]{1,0:T(8,128)(2,1)S(1)}, bf16[320,768]{1,0:T(8,128)(2,1)S(1)}, u32[]{:S(2)}, u32[]{:S(2)}) %collective-permute-start.17) | collective-permute-done | bytes 491552 | tf_op jit(solution)/shard_map/ppermute | solution.py:30
  179.5 5.7 %hidden.6 = (f32[320,768]{1,0:T(8,128)S(1)}, bf16[320,768]{1,0:T(8,128)(2,1)S(1)}, bf16[320,768]{1,0:T(8,128)(2,1)}, f32[320,768]{1,0:T(8,128)S(1)}, f32[320,768]{1,0:T(8,128)S(1)}, /*index=5*/f32[320,768]{1,0:T(8,128)S(1)}) custom-call(s32[4]{0:T(128)S(1)} %and_select_fusion.2.place, ...), custom_call_target="tpu_custom_call", output_to_operand_aliasing={{0}: (7, {}), {1}: (8, {}), {2}: (9, {}), {3}: (10, {}), {4... | custom-call | flops 2013265920 | bytes 7340032 | tf_op jit(solution)/shard_map/hidden/pallas_call | solution.py:174
  199.6 10.4 %back.2 = bf16[16,40,2048]{2,1,0:T(8,128)(2,1)} custom-call(s32[4]{0:T(128)S(1)} %and_select_fusion.2.place, s32[16]{0:T(128)S(1)} %add.135.target, bf16[320,512]{1,0:T(8,128)(2,1)S(1)} %collective-permute-done.19.rest_0_, bf16[320,512]{1,0:T(8,128)(2,1)S(1)} %collective-permute-done.24.rest_1_, bf16[320,512]{1,0:T(8,128)(2,1)S(1)} %collective-permute-done.25.rest_2_, ...), custom_call_target="tpu_custom_call" | custom-call | flops 5368709120 | bytes 14680064 | tf_op jit(solution)/shard_map/back/pallas_call | solution.py:230
  210.1 4.6 %all-to-all-start = ((bf16[16,40,2048]{2,1,0:T(8,128)(2,1)}), bf16[16,40,2048]{2,1,0:T(8,128)(2,1)}, u32[]{:S(2)}, u32[]{:S(2)}) async-start(bf16[16,40,2048]{2,1,0:T(8,128)(2,1)} %back.2), calls=%async_computation | async-start | bytes 5242880 | tf_op jit(solution)/shard_map/all_to_all | solution.py:278
  214.7 3.6 %collective-permute-done.40 = bf16[320,768]{1,0:T(8,128)(2,1)S(1)} collective-permute-done((bf16[320,768]{1,0:T(8,128)(2,1)}, bf16[320,768]{1,0:T(8,128)(2,1)S(1)}, u32[]{:S(2)}, u32[]{:S(2)}) %collective-permute-start.40) | collective-permute-done | bytes 491552 | tf_op jit(solution)/shard_map/ppermute | solution.py:30
  220.6 3.3 %collective-permute-start.41 = (bf16[320,512]{1,0:T(8,128)(2,1)S(1)}, bf16[320,512]{1,0:T(8,128)(2,1)S(1)}, u32[]{:S(2)}, u32[]{:S(2)}) collective-permute-start(bf16[320,512]{1,0:T(8,128)(2,1)S(1)} %pad_maximum_fusion.3.rest_7_), channel_id=1, source_target_pairs={{0,12},{4,0},{8,4},{12,8},{1,13},{5,1},{9,5},{13,9},{2,14},{6,2},{... | collective-permute-start | bytes 983048 | tf_op jit(solution)/shard_map/ppermute | solution.py:30
  233.9 3.5 %collective-permute-done.44.rest_5_ = bf16[320,512]{1,0:T(8,128)(2,1)S(1)} collective-permute-done((bf16[320,512]{1,0:T(8,128)(2,1)S(1)}, bf16[320,512]{1,0:T(8,128)(2,1)S(1)}, u32[]{:S(2)}, u32[]{:S(2)}) %collective-permute-start.44) | collective-permute-done | bytes 327712 | tf_op jit(solution)/shard_map/ppermute | solution.py:30
  237.4 4.8 %collective-permute-done.37.rest_0_ = bf16[320,512]{1,0:T(8,128)(2,1)S(1)} collective-permute-done((bf16[320,512]{1,0:T(8,128)(2,1)S(1)}, bf16[320,512]{1,0:T(8,128)(2,1)S(1)}, u32[]{:S(2)}, u32[]{:S(2)}) %collective-permute-start.37) | collective-permute-done | bytes 327712 | tf_op jit(solution)/shard_map/ppermute | solution.py:30
  242.2 9.9 %back.3 = bf16[16,40,2048]{2,1,0:T(8,128)(2,1)} custom-call(s32[4]{0:T(128)S(1)} %and_select_fusion.2.place, s32[16]{0:T(128)S(1)} %add.135.target, bf16[320,512]{1,0:T(8,128)(2,1)S(1)} %collective-permute-done.37.rest_0_, bf16[320,512]{1,0:T(8,128)(2,1)S(1)} %collective-permute-done.42.rest_1_, bf16[320,512]{1,0:T(8,128)(2,1)S(1)} %collective-permute-done.43.rest_2_, ...), custom_call_target="tpu_custom_call" | custom-call | flops 5368709120 | bytes 14680064 | tf_op jit(solution)/shard_map/back/pallas_call | solution.py:230
  252.1 6.1 %all-to-all-start.1 = ((bf16[16,40,2048]{2,1,0:T(8,128)(2,1)}), bf16[16,40,2048]{2,1,0:T(8,128)(2,1)S(1)}, u32[]{:S(2)}, u32[]{:S(2)}) async-start(bf16[16,40,2048]{2,1,0:T(8,128)(2,1)} %back.3), calls=%async_computation.1 | async-start | bytes 5242880 | tf_op jit(solution)/shard_map/all_to_all | solution.py:278
  260.4 19.8 %all-to-all-done.1 = bf16[16,40,2048]{2,1,0:T(8,128)(2,1)S(1)} async-done(((bf16[16,40,2048]{2,1,0:T(8,128)(2,1)}), bf16[16,40,2048]{2,1,0:T(8,128)(2,1)S(1)}, u32[]{:S(2)}, u32[]{:S(2)}) %all-to-all-start.1) | async-done | bytes 2621472 | tf_op jit(solution)/shard_map/all_to_all | solution.py:278
  (206 shorter events, 101.1 us)
Async XLA Ops:
  0.0 67.8 %collective-permute-start.12 = (bf16[2048,512]{1,0:T(8,128)(2,1)}, bf16[2048,512]{1,0:T(8,128)(2,1)}, u32[]{:S(2)}, u32[]{:S(2)}) collective-permute-start(bf16[2048,512]{1,0:T(8,128)(2,1)} %rest_8_.3), channel_id=1, source_target_pairs={{0,1},{1,0},{2,3},{3,2},{4,5},{5,4},{6,7},{7,6},{8,9},{9,8},{10,11... | collective-permute-start | bytes 6291464 | tf_op jit(solution)/shard_map/ppermute | solution.py:283
  0.0 67.8 %collective-permute-start.13 = (bf16[2048,512]{1,0:T(8,128)(2,1)}, bf16[2048,512]{1,0:T(8,128)(2,1)}, u32[]{:S(2)}, u32[]{:S(2)}) collective-permute-start(bf16[2048,512]{1,0:T(8,128)(2,1)} %rest_10_.3), channel_id=1, source_target_pairs={{0,1},{1,0},{2,3},{3,2},{4,5},{5,4},{6,7},{7,6},{8,9},{9,8},{10,11... | collective-permute-start | bytes 6291464 | tf_op jit(solution)/shard_map/ppermute | solution.py:283
  4.7 90.1 %collective-permute-start.6 = (bf16[512,2048]{1,0:T(8,128)(2,1)}, bf16[512,2048]{1,0:T(8,128)(2,1)}, u32[]{:S(2)}, u32[]{:S(2)}) collective-permute-start(bf16[512,2048]{1,0:T(8,128)(2,1)} %refs_4_.9), channel_id=1, source_target_pairs={{0,1},{1,0},{2,3},{3,2},{4,5},{5,4},{6,7},{7,6},{8,9},{9,8},{10,11... | collective-permute-start | bytes 6291464 | tf_op jit(solution)/shard_map/ppermute | solution.py:283
  39.6 21.6 %collective-permute-start.11 = (bf16[160,2048]{1,0:T(8,128)(2,1)}, bf16[160,2048]{1,0:T(8,128)(2,1)S(1)}, u32[]{:S(2)}, u32[]{:S(2)}) collective-permute-start(bf16[160,2048]{1,0:T(8,128)(2,1)} %get-tuple-element.46.refs_0_), channel_id=1, source_target_pairs={{0,66},{64,0},{2,64},{66,2},{1,67},{65,1},{3,65},{67,3},{4,70},{68... | collective-permute-start | bytes 1966088 | tf_op jit(solution)/shard_map/ppermute | solution.py:29
  55.9 27.9 %collective-permute-start.14 = (bf16[160,2048]{1,0:T(8,128)(2,1)}, bf16[160,2048]{1,0:T(8,128)(2,1)}, u32[]{:S(2)}, u32[]{:S(2)}) collective-permute-start(bf16[160,2048]{1,0:T(8,128)(2,1)} %get-tuple-element.46.refs_0_), channel_id=1, source_target_pairs={{0,2},{64,66},{2,0},{66,64},{1,3},{65,67},{3,1},{67,65},{4,6},{68,... | collective-permute-start | bytes 1966088 | tf_op jit(solution)/shard_map/ppermute | solution.py:29
  62.0 32.7 %collective-permute-start.3 = (bf16[160,2048]{1,0:T(8,128)(2,1)S(1)}, bf16[160,2048]{1,0:T(8,128)(2,1)S(1)}, u32[]{:S(2)}, u32[]{:S(2)}) collective-permute-start(bf16[160,2048]{1,0:T(8,128)(2,1)S(1)} %get-tuple-element.45.refs_0_), channel_id=1, source_target_pairs={{0,16},{16,32},{32,48},{48,0},{1,17},{17,33},{33,49},{49,1},{2,18}... | collective-permute-start | bytes 1966088 | tf_op jit(solution)/shard_map/ppermute | solution.py:30
  67.8 26.9 %collective-permute-start.4 = (bf16[160,2048]{1,0:T(8,128)(2,1)S(1)}, bf16[160,2048]{1,0:T(8,128)(2,1)S(1)}, u32[]{:S(2)}, u32[]{:S(2)}) collective-permute-start(bf16[160,2048]{1,0:T(8,128)(2,1)S(1)} %get-tuple-element.45.refs_0_), channel_id=1, source_target_pairs={{0,48},{16,0},{32,16},{48,32},{1,49},{17,1},{33,17},{49,33},{2,50}... | collective-permute-start | bytes 1966088 | tf_op jit(solution)/shard_map/ppermute | solution.py:30
  67.8 26.9 %collective-permute-start.5 = (bf16[160,2048]{1,0:T(8,128)(2,1)S(1)}, bf16[160,2048]{1,0:T(8,128)(2,1)S(1)}, u32[]{:S(2)}, u32[]{:S(2)}) collective-permute-start(bf16[160,2048]{1,0:T(8,128)(2,1)S(1)} %get-tuple-element.45.refs_0_), channel_id=1, source_target_pairs={{0,32},{16,48},{32,0},{48,16},{1,33},{17,49},{33,1},{49,17},{2,34}... | collective-permute-start | bytes 1966088 | tf_op jit(solution)/shard_map/ppermute | solution.py:30
  83.9 35.7 %collective-permute-start.30 = (bf16[160,2048]{1,0:T(8,128)(2,1)}, bf16[160,2048]{1,0:T(8,128)(2,1)}, u32[]{:S(2)}, u32[]{:S(2)}) collective-permute-start(bf16[160,2048]{1,0:T(8,128)(2,1)} %get-tuple-element.68.refs_0_), channel_id=1, source_target_pairs={{0,64},{64,2},{2,66},{66,0},{1,65},{65,3},{3,67},{67,1},{4,68},{68... | collective-permute-start | bytes 1966088 | tf_op jit(solution)/shard_map/ppermute | solution.py:29
  98.3 23.5 %collective-permute-start.21 = (bf16[320,768]{1,0:T(8,128)(2,1)S(1)}, bf16[320,768]{1,0:T(8,128)(2,1)}, u32[]{:S(2)}, u32[]{:S(2)}) collective-permute-start(bf16[320,768]{1,0:T(8,128)(2,1)S(1)} %get-tuple-element.66), channel_id=1, source_target_pairs={{0,12},{4,0},{8,4},{12,8},{1,13},{5,1},{9,5},{13,9},{2,14},{6,2},{... | collective-permute-start | bytes 1474568 | tf_op jit(solution)/shard_map/ppermute | solution.py:30
  101.3 24.0 %collective-permute-start.31 = (bf16[160,2048]{1,0:T(8,128)(2,1)}, bf16[160,2048]{1,0:T(8,128)(2,1)S(1)}, u32[]{:S(2)}, u32[]{:S(2)}) collective-permute-start(bf16[160,2048]{1,0:T(8,128)(2,1)} %get-tuple-element.68.refs_0_), channel_id=1, source_target_pairs={{0,66},{64,0},{2,64},{66,2},{1,67},{65,1},{3,65},{67,3},{4,70},{68... | collective-permute-start | bytes 1966088 | tf_op jit(solution)/shard_map/ppermute | solution.py:29
  102.9 22.5 %collective-permute-start.32 = (bf16[160,2048]{1,0:T(8,128)(2,1)}, bf16[160,2048]{1,0:T(8,128)(2,1)S(1)}, u32[]{:S(2)}, u32[]{:S(2)}) collective-permute-start(bf16[160,2048]{1,0:T(8,128)(2,1)} %get-tuple-element.68.refs_0_), channel_id=1, source_target_pairs={{0,2},{64,66},{2,0},{66,64},{1,3},{65,67},{3,1},{67,65},{4,6},{68,... | collective-permute-start | bytes 1966088 | tf_op jit(solution)/shard_map/ppermute | solution.py:29
  104.3 21.7 %collective-permute-start.27 = (bf16[160,2048]{1,0:T(8,128)(2,1)S(1)}, bf16[160,2048]{1,0:T(8,128)(2,1)S(1)}, u32[]{:S(2)}, u32[]{:S(2)}) collective-permute-start(bf16[160,2048]{1,0:T(8,128)(2,1)S(1)} %get-tuple-element.67.refs_0_), channel_id=1, source_target_pairs={{0,16},{16,32},{32,48},{48,0},{1,17},{17,33},{33,49},{49,1},{2,18}... | collective-permute-start | bytes 1966088 | tf_op jit(solution)/shard_map/ppermute | solution.py:30
  125.3 26.1 %collective-permute-start.20 = (bf16[320,768]{1,0:T(8,128)(2,1)}, bf16[320,768]{1,0:T(8,128)(2,1)S(1)}, u32[]{:S(2)}, u32[]{:S(2)}) collective-permute-start(bf16[320,768]{1,0:T(8,128)(2,1)} %get-tuple-element.64), channel_id=1, source_target_pairs={{0,4},{4,8},{8,12},{12,0},{1,5},{5,9},{9,13},{13,1},{2,6},{6,10},{... | collective-permute-start | bytes 1474568 | tf_op jit(solution)/shard_map/ppermute | solution.py:30
  125.4 25.8 %collective-permute-start.16 = (bf16[320,768]{1,0:T(8,128)(2,1)S(1)}, bf16[320,768]{1,0:T(8,128)(2,1)S(1)}, u32[]{:S(2)}, u32[]{:S(2)}) collective-permute-start(bf16[320,768]{1,0:T(8,128)(2,1)S(1)} %copy-done.41), channel_id=1, source_target_pairs={{0,4},{4,8},{8,12},{12,0},{1,5},{5,9},{9,13},{13,1},{2,6},{6,10},{... | collective-permute-start | bytes 1474568 | tf_op jit(solution)/shard_map/ppermute | solution.py:30
  126.1 25.4 %collective-permute-start.22 = (bf16[320,768]{1,0:T(8,128)(2,1)S(1)}, bf16[320,768]{1,0:T(8,128)(2,1)S(1)}, u32[]{:S(2)}, u32[]{:S(2)}) collective-permute-start(bf16[320,768]{1,0:T(8,128)(2,1)S(1)} %add_convert_fusion.2), channel_id=1, source_target_pairs={{0,12},{4,0},{8,4},{12,8},{1,13},{5,1},{9,5},{13,9},{2,14},{6,2},{... | collective-permute-start | bytes 1474568 | tf_op jit(solution)/shard_map/ppermute | solution.py:30
  146.0 39.2 %collective-permute-start.39 = (bf16[320,768]{1,0:T(8,128)(2,1)}, bf16[320,768]{1,0:T(8,128)(2,1)}, u32[]{:S(2)}, u32[]{:S(2)}) collective-permute-start(bf16[320,768]{1,0:T(8,128)(2,1)} %get-tuple-element.84), channel_id=1, source_target_pairs={{0,12},{4,0},{8,4},{12,8},{1,13},{5,1},{9,5},{13,9},{2,14},{6,2},{... | collective-permute-start | bytes 1474568 | tf_op jit(solution)/shard_map/ppermute | solution.py:30
  151.3 41.1 %collective-permute-start.34 = (bf16[320,768]{1,0:T(8,128)(2,1)}, bf16[320,768]{1,0:T(8,128)(2,1)}, u32[]{:S(2)}, u32[]{:S(2)}) collective-permute-start(bf16[320,768]{1,0:T(8,128)(2,1)} %get-tuple-element.80), channel_id=1, source_target_pairs={{0,4},{4,8},{8,12},{12,0},{1,5},{5,9},{9,13},{13,1},{2,6},{6,10},{... | collective-permute-start | bytes 1474568 | tf_op jit(solution)/shard_map/ppermute | solution.py:30
  152.6 35.9 %collective-permute-start.23 = (bf16[320,512]{1,0:T(8,128)(2,1)}, bf16[320,512]{1,0:T(8,128)(2,1)}, u32[]{:S(2)}, u32[]{:S(2)}) collective-permute-start(bf16[320,512]{1,0:T(8,128)(2,1)} %pad_maximum_fusion.1.rest_7_), channel_id=1, source_target_pairs={{0,12},{4,0},{8,4},{12,8},{1,13},{5,1},{9,5},{13,9},{2,14},{6,2},{... | collective-permute-start | bytes 983048 | tf_op jit(solution)/shard_map/ppermute | solution.py:30
  192.4 22.3 %collective-permute-start.38 = (bf16[320,768]{1,0:T(8,128)(2,1)S(1)}, bf16[320,768]{1,0:T(8,128)(2,1)}, u32[]{:S(2)}, u32[]{:S(2)}) collective-permute-start(bf16[320,768]{1,0:T(8,128)(2,1)S(1)} %get-tuple-element.82), channel_id=1, source_target_pairs={{0,4},{4,8},{8,12},{12,0},{1,5},{5,9},{9,13},{13,1},{2,6},{6,10},{... | collective-permute-start | bytes 1474568 | tf_op jit(solution)/shard_map/ppermute | solution.py:30
  194.9 29.0 %collective-permute-start.33 = (bf16[320,768]{1,0:T(8,128)(2,1)}, bf16[320,768]{1,0:T(8,128)(2,1)}, u32[]{:S(2)}, u32[]{:S(2)}) collective-permute-start(bf16[320,768]{1,0:T(8,128)(2,1)} %get-tuple-element.76), channel_id=1, source_target_pairs={{0,12},{4,0},{8,4},{12,8},{1,13},{5,1},{9,5},{13,9},{2,14},{6,2},{... | collective-permute-start | bytes 1474568 | tf_op jit(solution)/shard_map/ppermute | solution.py:30
  199.2 24.7 %collective-permute-start.35 = (bf16[320,768]{1,0:T(8,128)(2,1)}, bf16[320,768]{1,0:T(8,128)(2,1)}, u32[]{:S(2)}, u32[]{:S(2)}) collective-permute-start(bf16[320,768]{1,0:T(8,128)(2,1)} %add_convert_fusion.1), channel_id=1, source_target_pairs={{0,4},{4,8},{8,12},{12,0},{1,5},{5,9},{9,13},{13,1},{2,6},{6,10},{... | collective-permute-start | bytes 1474568 | tf_op jit(solution)/shard_map/ppermute | solution.py:30
  210.1 42.0 %all-to-all-start = ((bf16[16,40,2048]{2,1,0:T(8,128)(2,1)}), bf16[16,40,2048]{2,1,0:T(8,128)(2,1)}, u32[]{:S(2)}, u32[]{:S(2)}) async-start(bf16[16,40,2048]{2,1,0:T(8,128)(2,1)} %back.2), calls=%async_computation | async-start | bytes 5242880 | tf_op jit(solution)/shard_map/all_to_all | solution.py:278
  252.1 28.2 %all-to-all-start.1 = ((bf16[16,40,2048]{2,1,0:T(8,128)(2,1)}), bf16[16,40,2048]{2,1,0:T(8,128)(2,1)S(1)}, u32[]{:S(2)}, u32[]{:S(2)}) async-start(bf16[16,40,2048]{2,1,0:T(8,128)(2,1)} %back.3), calls=%async_computation.1 | async-start | bytes 5242880 | tf_op jit(solution)/shard_map/all_to_all | solution.py:278
  (74 other events, 703.8 us)

commit v3 on v2

--- a/solution.py
+++ b/solution.py
@@ -34,13 +34,23 @@
     return [value] + [shift(value, axis, step) for step in STEPS[1:]]
 
 
-def join_kernel(rows, *refs):
-    pieces, outs = refs[:RING], refs[RING:]
-    for k in range(RING):
+def join_kernel(rows, own, *refs):
+    pieces, outs, sems = refs[: RING - 1], refs[RING - 1 : -1], refs[-1]
+    copies = []
+    at = 0
+    for n, (count, out) in enumerate(zip(rows, outs)):
+        copies.append(
+            pltpu.make_async_copy(own.at[pl.ds(at, count)], out.at[pl.ds(0, count)], sems.at[n])
+        )
+        copies[-1].start()
+        at += count
+    for k in range(1, RING):
         at = 0
         for count, out in zip(rows, outs):
-            out[k * count : (k + 1) * count] = pieces[k][at : at + count]
+            out[k * count : (k + 1) * count] = pieces[k - 1][at : at + count]
             at += count
+    for copy in copies:
+        copy.wait()
 
 
 def join(pieces):
@@ -48,8 +58,9 @@
     spec = pl.BlockSpec(memory_space=pltpu.VMEM)
     return pl.pallas_call(
         functools.partial(join_kernel, CHUNKS),
-        in_specs=[spec] * RING,
+        in_specs=[pl.BlockSpec(memory_space=pl.ANY)] + [spec] * (RING - 1),
         out_specs=[spec] * len(CHUNKS),
+        scratch_shapes=[pltpu.SemaphoreType.DMA((len(CHUNKS),))],
         out_shape=[jax.ShapeDtypeStruct((RING * rows, width), pieces[0].dtype) for rows in CHUNKS],
         cost_estimate=pl.CostEstimate(flops=1 << 20, bytes_accessed=3 << 20, transcendentals=0),
         compiler_params=pltpu.CompilerParams(vmem_limit_bytes=16 << 20),
@@ -234,7 +245,7 @@
         cost_estimate=pl.CostEstimate(
             flops=16 * half * width * span, bytes_accessed=14 << 20, transcendentals=0
         ),
-        compiler_params=pltpu.CompilerParams(vmem_limit_bytes=VMEM_LIMIT),
+        compiler_params=pltpu.CompilerParams(vmem_limit_bytes=30 << 20),
         name="back",
     )(place, target, *pieces, *gates, *ups)
 

time: 283 us -> 282 us (level)
    unnamed x102 -> x106, local copies, waits for them, and re-layouts: 25.8 us -> 26.5 us
where the time goes in v3:
time: 282 us; the launch traced here: 281 us
  waiting for transfers between devices  93.3 us (33%)
  starting transfers between devices  81.7 us (29%)
  Pallas kernels  64.8 us (23%)
  local copies, waits for them, and re-layouts  26.6 us (9%)
  other arithmetic  14 us (5%)
    ppermute x33, starting transfers between devices, shift(): lax.ppermute(value, axis, [(i, (i + step) % RING) for i in range(RING)])  51.7 us
    ppermute x33, waiting for transfers between devices, shift(): lax.ppermute(value, axis, [(i, (i + step) % RING) for i in range(RING)])  50.5 us
    unnamed x106, local copies, waits for them, and re-layouts  26.5 us
    pallas_call x3, Pallas kernels, pair_terms(): pl.pallas_call(functools.partial(pair_kernel, count=count, sides=tuple(si...  26.2 us
    ppermute x9, waiting for transfers between devices, shift(): return lax.ppermute(value, ('xl', 'xh'), pairs)  23 us
    all_to_all x2, waiting for transfers between devices, finish(): crossed = lax.all_to_all(partial_value, XZ, 0, 0)  19.8 us
    pallas_call x2, Pallas kernels, back_terms(): pl.pallas_call(back_kernel, grid_spec=grid_spec, out_shape=jax.ShapeDtype...  19.1 us
    ppermute x9, starting transfers between devices, shift(): return lax.ppermute(value, ('xl', 'xh'), pairs)  18.6 us
  transfers between devices with their start and end apart: 47, of which 13 were waited for; matrix products, arithmetic and copies ran while one was open for 5% of the time, Pallas kernels for 23%

profile of v3, /device:TPU:0, one launch (start us, length us, event | category | flops | bytes accessed | tf_op | source)
XLA Modules:
  0.0 280.9 jit_solution(8109920437432415430)
XLA Ops:
  4.7 8.2 %collective-permute-done.7.refs_0_ = bf16[80,2048]{1,0:T(8,128)(2,1)S(1)} collective-permute-done((bf16[80,2048]{1,0:T(8,128)(2,1)}, bf16[80,2048]{1,0:T(8,128)(2,1)S(1)}, u32[]{:S(2)}, u32[]{:S(2)}) %collective-permute-start.7) | collective-permute-done | bytes 327712 | tf_op jit(solution)/shard_map/ppermute | solution.py:30
  15.9 7.8 %collective-permute-done.9.refs_2_ = bf16[80,2048]{1,0:T(8,128)(2,1)S(1)} collective-permute-done((bf16[80,2048]{1,0:T(8,128)(2,1)}, bf16[80,2048]{1,0:T(8,128)(2,1)S(1)}, u32[]{:S(2)}, u32[]{:S(2)}) %collective-permute-start.9) | collective-permute-done | bytes 327712 | tf_op jit(solution)/shard_map/ppermute | solution.py:30
  29.8 9.8 %collective-permute-done.1.refs_1_ = bf16[80,2048]{1,0:T(8,128)(2,1)S(1)} collective-permute-done((bf16[80,2048]{1,0:T(8,128)(2,1)}, bf16[80,2048]{1,0:T(8,128)(2,1)S(1)}, u32[]{:S(2)}, u32[]{:S(2)}) %collective-permute-start.1) | collective-permute-done | bytes 327712 | tf_op jit(solution)/shard_map/ppermute | solution.py:29
  39.6 3.6 %collective-permute-start.11 = (bf16[160,2048]{1,0:T(8,128)(2,1)}, bf16[160,2048]{1,0:T(8,128)(2,1)S(1)}, u32[]{:S(2)}, u32[]{:S(2)}) collective-permute-start(bf16[160,2048]{1,0:T(8,128)(2,1)} %get-tuple-element.46.refs_0_), channel_id=1, source_target_pairs={{0,66},{64,0},{2,64},{66,2},{1,67},{65,1},{3,65},{67,3},{4,70},{68... | collective-permute-start | bytes 1966088 | tf_op jit(solution)/shard_map/ppermute | solution.py:29
  43.1 12.0 %collective-permute-done.10.refs_1_ = bf16[160,2048]{1,0:T(8,128)(2,1)S(1)} collective-permute-done((bf16[160,2048]{1,0:T(8,128)(2,1)}, bf16[160,2048]{1,0:T(8,128)(2,1)S(1)}, u32[]{:S(2)}, u32[]{:S(2)}) %collective-permute-start.10) | collective-permute-done | bytes 655392 | tf_op jit(solution)/shard_map/ppermute | solution.py:29
  62.0 5.8 %collective-permute-start.3 = (bf16[160,2048]{1,0:T(8,128)(2,1)S(1)}, bf16[160,2048]{1,0:T(8,128)(2,1)S(1)}, u32[]{:S(2)}, u32[]{:S(2)}) collective-permute-start(bf16[160,2048]{1,0:T(8,128)(2,1)S(1)} %get-tuple-element.45.refs_0_), channel_id=1, source_target_pairs={{0,16},{16,32},{32,48},{48,0},{1,17},{17,33},{33,49},{49,1},{2,18}... | collective-permute-start | bytes 1966088 | tf_op jit(solution)/shard_map/ppermute | solution.py:30
  72.1 9.0 %pair.3 = (bf16[320,768]{1,0:T(8,128)(2,1)S(1)}, bf16[320,768]{1,0:T(8,128)(2,1)S(1)}, f32[320,768]{1,0:T(8,128)S(1)}, bf16[320,768]{1,0:T(8,128)(2,1)}, bf16[32...) custom-call(s32[4]{0:T(128)S(1)} %and_select_fusion.2.place, ...), custom_call_target="tpu_custom_call" | custom-call | flops 4026531840 | bytes 14680064 | tf_op jit(solution)/shard_map/pair/pallas_call | solution.py:125
  83.8 4.4 %collective-permute-start.30 = (bf16[160,2048]{1,0:T(8,128)(2,1)}, bf16[160,2048]{1,0:T(8,128)(2,1)}, u32[]{:S(2)}, u32[]{:S(2)}) collective-permute-start(bf16[160,2048]{1,0:T(8,128)(2,1)} %get-tuple-element.68.refs_0_), channel_id=1, source_target_pairs={{0,64},{64,2},{2,66},{66,0},{1,65},{65,3},{3,67},{67,1},{4,68},{68... | collective-permute-start | bytes 1966088 | tf_op jit(solution)/shard_map/ppermute | solution.py:29
  88.3 6.5 %pair.4 = (bf16[320,768]{1,0:T(8,128)(2,1)S(1)}, bf16[320,768]{1,0:T(8,128)(2,1)}, f32[320,768]{1,0:T(8,128)S(1)}, f32[320,768]{1,0:T(8,128)S(1)}) custom-call(s32[4]{0:T(128)S(1)} %and_select_fusion.2.place, bf16[160,2048]{1,0:T(8,128)(2,1)} %collective-permute-done.14.refs_0_, ...), custom_call_target="tpu_custom_call", output_to_operand_aliasing={{0}: (6, {}), {1}: (7, {}), {2}: (8, {}), {3}: (9, {})} | custom-call | flops 1342177280 | bytes 14680064 | tf_op jit(solution)/shard_map/pair/pallas_call | solution.py:125
  112.1 5.7 %hidden.4 = (f32[320,768]{1,0:T(8,128)S(1)}, bf16[320,768]{1,0:T(8,128)(2,1)}, bf16[320,768]{1,0:T(8,128)(2,1)S(1)}, f32[320,768]{1,0:T(8,128)S(1)}, f32[320,768]{1,0:T(8,128)S(1)}, /*index=5*/f32[320,768]{1,0:T(8,128)S(1)}) custom-call(s32[4]{0:T(128)S(1)} %and_select_fusion.2.place, ...), custom_call_target="tpu_custom_call", output_to_operand_aliasing={{0}: (7, {}), {1}: (8, {}), {2}: (9, {}), {3}: (10, {}), {4... | custom-call | flops 2013265920 | bytes 7340032 | tf_op jit(solution)/shard_map/hidden/pallas_call | solution.py:185
  128.8 10.8 %pair.5 = (bf16[320,768]{1,0:T(8,128)(2,1)}, bf16[320,768]{1,0:T(8,128)(2,1)}, f32[320,768]{1,0:T(8,128)S(1)}, bf16[320,768]{1,0:T(8,128)(2,1)S(1)}, bf16[320,76...) custom-call(s32[4]{0:T(128)S(1)} %and_select_fusion.2.place, ...), custom_call_target="tpu_custom_call" | custom-call | flops 5368709120 | bytes 14680064 | tf_op jit(solution)/shard_map/pair/pallas_call | solution.py:125
  142.7 3.2 %hidden.7 = (bf16[320,768]{1,0:T(8,128)(2,1)}, bf16[320,768]{1,0:T(8,128)(2,1)}) custom-call(s32[4]{0:T(128)S(1)} %and_select_fusion.2.place, bf16[160,2048]{1,0:T(8,128)(2,1)S(1)} %get-tuple-element.67.refs_0_, bf16[160,2048]{1,0:T(8,128)(2,1)S(1)} %collective-permute-done.27.refs_1_, ...), custom_call_target="tpu_custom_call", output_to_operand_aliasing={{0}: (7, {}), {1}: (8, {})} | custom-call | flops 671088640 | bytes 7340032 | tf_op jit(solution)/shard_map/hidden/pallas_call | solution.py:185
  146.5 4.7 %collective-permute-done.16 = bf16[320,768]{1,0:T(8,128)(2,1)S(1)} collective-permute-done((bf16[320,768]{1,0:T(8,128)(2,1)S(1)}, bf16[320,768]{1,0:T(8,128)(2,1)S(1)}, u32[]{:S(2)}, u32[]{:S(2)}) %collective-permute-start.16) | collective-permute-done | bytes 491552 | tf_op jit(solution)/shard_map/ppermute | solution.py:30
  152.6 3.2 %collective-permute-start.23 = (bf16[320,512]{1,0:T(8,128)(2,1)}, bf16[320,512]{1,0:T(8,128)(2,1)}, u32[]{:S(2)}, u32[]{:S(2)}) collective-permute-start(bf16[320,512]{1,0:T(8,128)(2,1)} %pad_maximum_fusion.1.rest_7_), channel_id=1, source_target_pairs={{0,12},{4,0},{8,4},{12,8},{1,13},{5,1},{9,5},{13,9},{2,14},{6,2},{... | collective-permute-start | bytes 983048 | tf_op jit(solution)/shard_map/ppermute | solution.py:30
  155.8 16.4 %collective-permute-done.17 = bf16[320,768]{1,0:T(8,128)(2,1)S(1)} collective-permute-done((bf16[320,768]{1,0:T(8,128)(2,1)S(1)}, bf16[320,768]{1,0:T(8,128)(2,1)S(1)}, u32[]{:S(2)}, u32[]{:S(2)}) %collective-permute-start.17) | collective-permute-done | bytes 491552 | tf_op jit(solution)/shard_map/ppermute | solution.py:30
  179.4 5.8 %hidden.6 = (f32[320,768]{1,0:T(8,128)S(1)}, bf16[320,768]{1,0:T(8,128)(2,1)S(1)}, bf16[320,768]{1,0:T(8,128)(2,1)}, f32[320,768]{1,0:T(8,128)S(1)}, f32[320,768]{1,0:T(8,128)S(1)}, /*index=5*/f32[320,768]{1,0:T(8,128)S(1)}) custom-call(s32[4]{0:T(128)S(1)} %and_select_fusion.2.place, ...), custom_call_target="tpu_custom_call", output_to_operand_aliasing={{0}: (7, {}), {1}: (8, {}), {2}: (9, {}), {3}: (10, {}), {4... | custom-call | flops 2013265920 | bytes 7340032 | tf_op jit(solution)/shard_map/hidden/pallas_call | solution.py:185
  199.6 9.4 %back.2 = bf16[16,40,2048]{2,1,0:T(8,128)(2,1)S(1)} custom-call(s32[4]{0:T(128)S(1)} %and_select_fusion.2.place, s32[16]{0:T(128)S(1)} %add.135.target, bf16[320,512]{1,0:T(8,128)(2,1)S(1)} %collective-permute-done.19.rest_0_, bf16[320,512]{1,0:T(8,128)(2,1)S(1)} %collective-permute-done.24.rest_1_, bf16[320,512]{1,0:T(8,128)(2,1)S(1)} %collective-permute-done.25.rest_2_, ...), custom_call_target="tpu_custom_call" | custom-call | flops 5368709120 | bytes 14680064 | tf_op jit(solution)/shard_map/back/pallas_call | solution.py:241
  210.6 4.6 %all-to-all-start = ((bf16[16,40,2048]{2,1,0:T(8,128)(2,1)}), bf16[16,40,2048]{2,1,0:T(8,128)(2,1)}, u32[]{:S(2)}, u32[]{:S(2)}) async-start(bf16[16,40,2048]{2,1,0:T(8,128)(2,1)} %copy-done.33), calls=%async_computation | async-start | bytes 5242880 | tf_op jit(solution)/shard_map/all_to_all | solution.py:289
  219.6 3.6 %collective-permute-start.41 = (bf16[320,512]{1,0:T(8,128)(2,1)S(1)}, bf16[320,512]{1,0:T(8,128)(2,1)S(1)}, u32[]{:S(2)}, u32[]{:S(2)}) collective-permute-start(bf16[320,512]{1,0:T(8,128)(2,1)S(1)} %pad_maximum_fusion.3.rest_7_), channel_id=1, source_target_pairs={{0,12},{4,0},{8,4},{12,8},{1,13},{5,1},{9,5},{13,9},{2,14},{6,2},{... | collective-permute-start | bytes 983048 | tf_op jit(solution)/shard_map/ppermute | solution.py:30
  233.2 3.5 %collective-permute-done.44.rest_5_ = bf16[320,512]{1,0:T(8,128)(2,1)S(1)} collective-permute-done((bf16[320,512]{1,0:T(8,128)(2,1)S(1)}, bf16[320,512]{1,0:T(8,128)(2,1)S(1)}, u32[]{:S(2)}, u32[]{:S(2)}) %collective-permute-start.44) | collective-permute-done | bytes 327712 | tf_op jit(solution)/shard_map/ppermute | solution.py:30
  236.7 4.8 %collective-permute-done.37.rest_0_ = bf16[320,512]{1,0:T(8,128)(2,1)S(1)} collective-permute-done((bf16[320,512]{1,0:T(8,128)(2,1)S(1)}, bf16[320,512]{1,0:T(8,128)(2,1)S(1)}, u32[]{:S(2)}, u32[]{:S(2)}) %collective-permute-start.37) | collective-permute-done | bytes 327712 | tf_op jit(solution)/shard_map/ppermute | solution.py:30
  241.5 9.7 %back.3 = bf16[16,40,2048]{2,1,0:T(8,128)(2,1)} custom-call(s32[4]{0:T(128)S(1)} %and_select_fusion.2.place, s32[16]{0:T(128)S(1)} %add.135.target, bf16[320,512]{1,0:T(8,128)(2,1)S(1)} %collective-permute-done.37.rest_0_, bf16[320,512]{1,0:T(8,128)(2,1)S(1)} %collective-permute-done.42.rest_1_, bf16[320,512]{1,0:T(8,128)(2,1)S(1)} %collective-permute-done.43.rest_2_, ...), custom_call_target="tpu_custom_call" | custom-call | flops 5368709120 | bytes 14680064 | tf_op jit(solution)/shard_map/back/pallas_call | solution.py:241
  251.2 6.3 %all-to-all-start.1 = ((bf16[16,40,2048]{2,1,0:T(8,128)(2,1)}), bf16[16,40,2048]{2,1,0:T(8,128)(2,1)S(1)}, u32[]{:S(2)}, u32[]{:S(2)}) async-start(bf16[16,40,2048]{2,1,0:T(8,128)(2,1)} %back.3), calls=%async_computation.1 | async-start | bytes 5242880 | tf_op jit(solution)/shard_map/all_to_all | solution.py:289
  259.8 19.8 %all-to-all-done.1 = bf16[16,40,2048]{2,1,0:T(8,128)(2,1)S(1)} async-done(((bf16[16,40,2048]{2,1,0:T(8,128)(2,1)}), bf16[16,40,2048]{2,1,0:T(8,128)(2,1)S(1)}, u32[]{:S(2)}, u32[]{:S(2)}) %all-to-all-start.1) | async-done | bytes 2621472 | tf_op jit(solution)/shard_map/all_to_all | solution.py:289
  (210 shorter events, 101.9 us)
Async XLA Ops:
  0.0 67.8 %collective-permute-start.12 = (bf16[2048,512]{1,0:T(8,128)(2,1)}, bf16[2048,512]{1,0:T(8,128)(2,1)}, u32[]{:S(2)}, u32[]{:S(2)}) collective-permute-start(bf16[2048,512]{1,0:T(8,128)(2,1)} %rest_8_.3), channel_id=1, source_target_pairs={{0,1},{1,0},{2,3},{3,2},{4,5},{5,4},{6,7},{7,6},{8,9},{9,8},{10,11... | collective-permute-start | bytes 6291464 | tf_op jit(solution)/shard_map/ppermute | solution.py:294
  0.0 67.8 %collective-permute-start.13 = (bf16[2048,512]{1,0:T(8,128)(2,1)}, bf16[2048,512]{1,0:T(8,128)(2,1)}, u32[]{:S(2)}, u32[]{:S(2)}) collective-permute-start(bf16[2048,512]{1,0:T(8,128)(2,1)} %rest_10_.3), channel_id=1, source_target_pairs={{0,1},{1,0},{2,3},{3,2},{4,5},{5,4},{6,7},{7,6},{8,9},{9,8},{10,11... | collective-permute-start | bytes 6291464 | tf_op jit(solution)/shard_map/ppermute | solution.py:294
  4.7 90.1 %collective-permute-start.6 = (bf16[512,2048]{1,0:T(8,128)(2,1)}, bf16[512,2048]{1,0:T(8,128)(2,1)}, u32[]{:S(2)}, u32[]{:S(2)}) collective-permute-start(bf16[512,2048]{1,0:T(8,128)(2,1)} %refs_4_.9), channel_id=1, source_target_pairs={{0,1},{1,0},{2,3},{3,2},{4,5},{5,4},{6,7},{7,6},{8,9},{9,8},{10,11... | collective-permute-start | bytes 6291464 | tf_op jit(solution)/shard_map/ppermute | solution.py:294
  39.6 21.6 %collective-permute-start.11 = (bf16[160,2048]{1,0:T(8,128)(2,1)}, bf16[160,2048]{1,0:T(8,128)(2,1)S(1)}, u32[]{:S(2)}, u32[]{:S(2)}) collective-permute-start(bf16[160,2048]{1,0:T(8,128)(2,1)} %get-tuple-element.46.refs_0_), channel_id=1, source_target_pairs={{0,66},{64,0},{2,64},{66,2},{1,67},{65,1},{3,65},{67,3},{4,70},{68... | collective-permute-start | bytes 1966088 | tf_op jit(solution)/shard_map/ppermute | solution.py:29
  55.9 27.9 %collective-permute-start.14 = (bf16[160,2048]{1,0:T(8,128)(2,1)}, bf16[160,2048]{1,0:T(8,128)(2,1)}, u32[]{:S(2)}, u32[]{:S(2)}) collective-permute-start(bf16[160,2048]{1,0:T(8,128)(2,1)} %get-tuple-element.46.refs_0_), channel_id=1, source_target_pairs={{0,2},{64,66},{2,0},{66,64},{1,3},{65,67},{3,1},{67,65},{4,6},{68,... | collective-permute-start | bytes 1966088 | tf_op jit(solution)/shard_map/ppermute | solution.py:29
  62.0 32.7 %collective-permute-start.3 = (bf16[160,2048]{1,0:T(8,128)(2,1)S(1)}, bf16[160,2048]{1,0:T(8,128)(2,1)S(1)}, u32[]{:S(2)}, u32[]{:S(2)}) collective-permute-start(bf16[160,2048]{1,0:T(8,128)(2,1)S(1)} %get-tuple-element.45.refs_0_), channel_id=1, source_target_pairs={{0,16},{16,32},{32,48},{48,0},{1,17},{17,33},{33,49},{49,1},{2,18}... | collective-permute-start | bytes 1966088 | tf_op jit(solution)/shard_map/ppermute | solution.py:30
  67.8 26.9 %collective-permute-start.4 = (bf16[160,2048]{1,0:T(8,128)(2,1)S(1)}, bf16[160,2048]{1,0:T(8,128)(2,1)S(1)}, u32[]{:S(2)}, u32[]{:S(2)}) collective-permute-start(bf16[160,2048]{1,0:T(8,128)(2,1)S(1)} %get-tuple-element.45.refs_0_), channel_id=1, source_target_pairs={{0,48},{16,0},{32,16},{48,32},{1,49},{17,1},{33,17},{49,33},{2,50}... | collective-permute-start | bytes 1966088 | tf_op jit(solution)/shard_map/ppermute | solution.py:30
  67.8 26.9 %collective-permute-start.5 = (bf16[160,2048]{1,0:T(8,128)(2,1)S(1)}, bf16[160,2048]{1,0:T(8,128)(2,1)S(1)}, u32[]{:S(2)}, u32[]{:S(2)}) collective-permute-start(bf16[160,2048]{1,0:T(8,128)(2,1)S(1)} %get-tuple-element.45.refs_0_), channel_id=1, source_target_pairs={{0,32},{16,48},{32,0},{48,16},{1,33},{17,49},{33,1},{49,17},{2,34}... | collective-permute-start | bytes 1966088 | tf_op jit(solution)/shard_map/ppermute | solution.py:30
  83.8 35.7 %collective-permute-start.30 = (bf16[160,2048]{1,0:T(8,128)(2,1)}, bf16[160,2048]{1,0:T(8,128)(2,1)}, u32[]{:S(2)}, u32[]{:S(2)}) collective-permute-start(bf16[160,2048]{1,0:T(8,128)(2,1)} %get-tuple-element.68.refs_0_), channel_id=1, source_target_pairs={{0,64},{64,2},{2,66},{66,0},{1,65},{65,3},{3,67},{67,1},{4,68},{68... | collective-permute-start | bytes 1966088 | tf_op jit(solution)/shard_map/ppermute | solution.py:29
  98.3 23.5 %collective-permute-start.21 = (bf16[320,768]{1,0:T(8,128)(2,1)S(1)}, bf16[320,768]{1,0:T(8,128)(2,1)}, u32[]{:S(2)}, u32[]{:S(2)}) collective-permute-start(bf16[320,768]{1,0:T(8,128)(2,1)S(1)} %get-tuple-element.66), channel_id=1, source_target_pairs={{0,12},{4,0},{8,4},{12,8},{1,13},{5,1},{9,5},{13,9},{2,14},{6,2},{... | collective-permute-start | bytes 1474568 | tf_op jit(solution)/shard_map/ppermute | solution.py:30
  101.3 23.9 %collective-permute-start.31 = (bf16[160,2048]{1,0:T(8,128)(2,1)}, bf16[160,2048]{1,0:T(8,128)(2,1)S(1)}, u32[]{:S(2)}, u32[]{:S(2)}) collective-permute-start(bf16[160,2048]{1,0:T(8,128)(2,1)} %get-tuple-element.68.refs_0_), channel_id=1, source_target_pairs={{0,66},{64,0},{2,64},{66,2},{1,67},{65,1},{3,65},{67,3},{4,70},{68... | collective-permute-start | bytes 1966088 | tf_op jit(solution)/shard_map/ppermute | solution.py:29
  102.9 22.5 %collective-permute-start.32 = (bf16[160,2048]{1,0:T(8,128)(2,1)}, bf16[160,2048]{1,0:T(8,128)(2,1)S(1)}, u32[]{:S(2)}, u32[]{:S(2)}) collective-permute-start(bf16[160,2048]{1,0:T(8,128)(2,1)} %get-tuple-element.68.refs_0_), channel_id=1, source_target_pairs={{0,2},{64,66},{2,0},{66,64},{1,3},{65,67},{3,1},{67,65},{4,6},{68,... | collective-permute-start | bytes 1966088 | tf_op jit(solution)/shard_map/ppermute | solution.py:29
  104.3 21.7 %collective-permute-start.27 = (bf16[160,2048]{1,0:T(8,128)(2,1)S(1)}, bf16[160,2048]{1,0:T(8,128)(2,1)S(1)}, u32[]{:S(2)}, u32[]{:S(2)}) collective-permute-start(bf16[160,2048]{1,0:T(8,128)(2,1)S(1)} %get-tuple-element.67.refs_0_), channel_id=1, source_target_pairs={{0,16},{16,32},{32,48},{48,0},{1,17},{17,33},{33,49},{49,1},{2,18}... | collective-permute-start | bytes 1966088 | tf_op jit(solution)/shard_map/ppermute | solution.py:30
  125.3 26.1 %collective-permute-start.20 = (bf16[320,768]{1,0:T(8,128)(2,1)}, bf16[320,768]{1,0:T(8,128)(2,1)S(1)}, u32[]{:S(2)}, u32[]{:S(2)}) collective-permute-start(bf16[320,768]{1,0:T(8,128)(2,1)} %get-tuple-element.64), channel_id=1, source_target_pairs={{0,4},{4,8},{8,12},{12,0},{1,5},{5,9},{9,13},{13,1},{2,6},{6,10},{... | collective-permute-start | bytes 1474568 | tf_op jit(solution)/shard_map/ppermute | solution.py:30
  125.4 25.8 %collective-permute-start.16 = (bf16[320,768]{1,0:T(8,128)(2,1)S(1)}, bf16[320,768]{1,0:T(8,128)(2,1)S(1)}, u32[]{:S(2)}, u32[]{:S(2)}) collective-permute-start(bf16[320,768]{1,0:T(8,128)(2,1)S(1)} %copy-done.44), channel_id=1, source_target_pairs={{0,4},{4,8},{8,12},{12,0},{1,5},{5,9},{9,13},{13,1},{2,6},{6,10},{... | collective-permute-start | bytes 1474568 | tf_op jit(solution)/shard_map/ppermute | solution.py:30
  126.0 25.4 %collective-permute-start.22 = (bf16[320,768]{1,0:T(8,128)(2,1)S(1)}, bf16[320,768]{1,0:T(8,128)(2,1)S(1)}, u32[]{:S(2)}, u32[]{:S(2)}) collective-permute-start(bf16[320,768]{1,0:T(8,128)(2,1)S(1)} %add_convert_fusion.2), channel_id=1, source_target_pairs={{0,12},{4,0},{8,4},{12,8},{1,13},{5,1},{9,5},{13,9},{2,14},{6,2},{... | collective-permute-start | bytes 1474568 | tf_op jit(solution)/shard_map/ppermute | solution.py:30
  146.0 39.2 %collective-permute-start.39 = (bf16[320,768]{1,0:T(8,128)(2,1)}, bf16[320,768]{1,0:T(8,128)(2,1)}, u32[]{:S(2)}, u32[]{:S(2)}) collective-permute-start(bf16[320,768]{1,0:T(8,128)(2,1)} %get-tuple-element.84), channel_id=1, source_target_pairs={{0,12},{4,0},{8,4},{12,8},{1,13},{5,1},{9,5},{13,9},{2,14},{6,2},{... | collective-permute-start | bytes 1474568 | tf_op jit(solution)/shard_map/ppermute | solution.py:30
  151.2 41.1 %collective-permute-start.34 = (bf16[320,768]{1,0:T(8,128)(2,1)}, bf16[320,768]{1,0:T(8,128)(2,1)}, u32[]{:S(2)}, u32[]{:S(2)}) collective-permute-start(bf16[320,768]{1,0:T(8,128)(2,1)} %get-tuple-element.80), channel_id=1, source_target_pairs={{0,4},{4,8},{8,12},{12,0},{1,5},{5,9},{9,13},{13,1},{2,6},{6,10},{... | collective-permute-start | bytes 1474568 | tf_op jit(solution)/shard_map/ppermute | solution.py:30
  152.6 35.9 %collective-permute-start.23 = (bf16[320,512]{1,0:T(8,128)(2,1)}, bf16[320,512]{1,0:T(8,128)(2,1)}, u32[]{:S(2)}, u32[]{:S(2)}) collective-permute-start(bf16[320,512]{1,0:T(8,128)(2,1)} %pad_maximum_fusion.1.rest_7_), channel_id=1, source_target_pairs={{0,12},{4,0},{8,4},{12,8},{1,13},{5,1},{9,5},{13,9},{2,14},{6,2},{... | collective-permute-start | bytes 983048 | tf_op jit(solution)/shard_map/ppermute | solution.py:30
  192.4 22.8 %collective-permute-start.38 = (bf16[320,768]{1,0:T(8,128)(2,1)S(1)}, bf16[320,768]{1,0:T(8,128)(2,1)}, u32[]{:S(2)}, u32[]{:S(2)}) collective-permute-start(bf16[320,768]{1,0:T(8,128)(2,1)S(1)} %get-tuple-element.82), channel_id=1, source_target_pairs={{0,4},{4,8},{8,12},{12,0},{1,5},{5,9},{9,13},{13,1},{2,6},{6,10},{... | collective-permute-start | bytes 1474568 | tf_op jit(solution)/shard_map/ppermute | solution.py:30
  194.9 28.3 %collective-permute-start.33 = (bf16[320,768]{1,0:T(8,128)(2,1)}, bf16[320,768]{1,0:T(8,128)(2,1)}, u32[]{:S(2)}, u32[]{:S(2)}) collective-permute-start(bf16[320,768]{1,0:T(8,128)(2,1)} %get-tuple-element.76), channel_id=1, source_target_pairs={{0,12},{4,0},{8,4},{12,8},{1,13},{5,1},{9,5},{13,9},{2,14},{6,2},{... | collective-permute-start | bytes 1474568 | tf_op jit(solution)/shard_map/ppermute | solution.py:30
  199.2 24.0 %collective-permute-start.35 = (bf16[320,768]{1,0:T(8,128)(2,1)}, bf16[320,768]{1,0:T(8,128)(2,1)}, u32[]{:S(2)}, u32[]{:S(2)}) collective-permute-start(bf16[320,768]{1,0:T(8,128)(2,1)} %add_convert_fusion.1), channel_id=1, source_target_pairs={{0,4},{4,8},{8,12},{12,0},{1,5},{5,9},{9,13},{13,1},{2,6},{6,10},{... | collective-permute-start | bytes 1474568 | tf_op jit(solution)/shard_map/ppermute | solution.py:30
  210.6 40.6 %all-to-all-start = ((bf16[16,40,2048]{2,1,0:T(8,128)(2,1)}), bf16[16,40,2048]{2,1,0:T(8,128)(2,1)}, u32[]{:S(2)}, u32[]{:S(2)}) async-start(bf16[16,40,2048]{2,1,0:T(8,128)(2,1)} %copy-done.33), calls=%async_computation | async-start | bytes 5242880 | tf_op jit(solution)/shard_map/all_to_all | solution.py:289
  251.2 28.4 %all-to-all-start.1 = ((bf16[16,40,2048]{2,1,0:T(8,128)(2,1)}), bf16[16,40,2048]{2,1,0:T(8,128)(2,1)S(1)}, u32[]{:S(2)}, u32[]{:S(2)}) async-start(bf16[16,40,2048]{2,1,0:T(8,128)(2,1)} %back.3), calls=%async_computation.1 | async-start | bytes 5242880 | tf_op jit(solution)/shard_map/all_to_all | solution.py:289
  (76 other events, 741.1 us)
